TPU v7x, 512 devices: a whole 4x4x16 slice. The times are simulated.
512 devices in a mesh: samp: 128 (over z, y, core), snp: 4 (over x).
Axes of the slice: x: 4, y: 4, z: 16, core: 2. Of those that a mesh axis runs over, the one named last changes fastest.
Arguments:
- geno_words: int32 [32768, 1024], P('samp', 'snp'), may hold values from -2147483648 to 2147483647, as said below
- counts: int32 [32768], P('samp'), may hold values from 0 to 4, as said below
- probes: bfloat16 [32768, 64], P('samp'), may hold values from -6 to 6
- phenotype: float32 [32768], P('samp'), may hold values from -6 to 6
- tile_comp: int32 [128], replicated, may hold values from 0 to 7, as said below
Outputs:
- images: bfloat16 [32768, 512], P(('samp', 'snp'))
- traces: float32 [8, 8], replicated
- yky: float32 [8], replicated
Inputs may be any that keep to these rules, and one draw needn't show every extreme that they name: `geno_words`: each word packs sixteen dosages of one sample in 2-bit fields as step one reads them; every field holds 0, 1 or 2. `counts`: at least one sample has a count of one or more. `tile_comp`: every component owns at least one tile.
All inputs are finite; a program needn't handle non-finite values.
Results may differ from a plain program's by a relative error of at most 0.015.
Values may be sent and summed in bfloat16 or wider, within the bound.
No kernel may reach another device: no remote copies, remote signals or barrier semaphores. Data moves between devices by JAX's collectives and lax.ppermute only.
A program may use at most 64 MiB of HBM per device.

v0:
```python
import jax
import jax.numpy as jnp
from jax import lax
from jax.sharding import Mesh
from jax.sharding import PartitionSpec as P

SNPS = 16384
COMPS = 8
SAMP = ("samp_0", "samp_1", "samp_2")
SAMP_SNP = ("samp_0", "samp_1", "samp_2", "snp")


EPSILON = 1e-05


def cut_along(shard, dim, size):
    before, after = (shard.shape[:dim], shard.shape[dim + 1 :])
    return jnp.moveaxis(shard.reshape(*before, size, -1, *after), dim, 0)


def sent_and_summed(shard, axis, dim):
    size = lax.axis_size(axis)
    blocks = lax.all_to_all(cut_along(shard, dim, size), axis, 0, 0, tiled=True)
    return jnp.sum(blocks, axis=0)


def sum_by_axis(shard, axes, dim):
    far, near = axes
    blocks = cut_along(shard, dim, lax.axis_size(far))
    nearer = sent_and_summed(blocks, near, dim + 1)
    arrived = lax.all_to_all(nearer, far, split_axis=0, concat_axis=0, tiled=True)
    return arrived.sum(axis=0)


def padded_to(lines, size):
    spare = -len(lines) % size
    return jnp.pad(lines, [(0, spare)] + [(0, 0)] * (lines.ndim - 1))


def sent_to_all(shard, axis):
    size = lax.axis_size(axis)
    return lax.all_to_all(
        jnp.broadcast_to(shard[None], (size, *shard.shape)), axis, 0, 0, tiled=True
    )


def joined_along(blocks, dim):
    blocks = jnp.moveaxis(blocks, 0, dim)
    lengths = blocks.shape
    return blocks.reshape(*lengths[:dim], lengths[dim] * lengths[dim + 1], *lengths[dim + 2 :])


def gathered_by_axis(shard, axes, dim):
    far, near = axes
    initial = sent_to_all(shard, far)
    blocks = jnp.swapaxes(sent_to_all(initial, near), 0, 1)
    return joined_along(blocks.reshape(-1, *shard.shape), dim)


def sum_by_parts(shard, axes):
    own = sum_by_axis(padded_to(shard, lax.axis_size(axes[0]) * lax.axis_size(axes[1])), axes, 0)
    whole = gathered_by_axis(own, axes, 0)
    return whole[: len(shard)].reshape(shard.shape)


def packed_total(arrays, axis):
    ravelled, at, done = (jnp.concatenate([a.reshape(-1) for a in arrays]), 0, [])
    total = sum_by_parts(ravelled, axis)
    for a in arrays:
        done.append(total[at : at + a.size].reshape(a.shape))
        at += a.size
    return tuple(done)


def of_everyone(shard, axis):
    everything = sent_to_all(shard, axis)
    return jnp.sum(everything, axis=0)


def one_axis_at_a_time(shard, axes):
    far, near = axes
    return of_everyone(of_everyone(shard, near), far)


def unpack_rows(packed):
    height = packed.shape[0]
    grouped = packed.reshape(height, -1, 1, 128)
    shifts = 2 * jnp.arange(16, dtype=jnp.int32).reshape(1, 1, 16, 1)
    fields = jnp.right_shift(grouped, shifts) & 3
    return fields.reshape(height, -1).astype(jnp.bfloat16)


def block_number(row_count):
    number = 1
    while row_count // number > 768 or row_count % number != 0:
        number = number + 1
    return number


def finish(panel_part, moment_part, totals, inverse, member):
    weight_total = totals[0]
    pheno_total = totals[1]
    probe_total = totals[2:]
    average = moment_part[0] / weight_total
    second = moment_part[1] / weight_total
    spread = 1.0 / jnp.sqrt(second - average * average + EPSILON)
    unit_panel = spread[:, None] * (panel_part - average[:, None] * probe_total[None, :])
    pheno_unit = spread * (moment_part[2] - average * pheno_total)
    coefficients = (spread[:, None] * unit_panel * inverse[:, None]).astype(jnp.bfloat16)
    energy = jnp.sum(member * (pheno_unit * pheno_unit * inverse)[:, None], axis=0)
    return (average, coefficients, energy)


def on_device(geno_words, counts, probes, phenotype, tile_comp):
    height = geno_words.shape[0]
    snp_local = geno_words.shape[1] * 16
    tile_local = snp_local // 128
    probe_count = probes.shape[1]
    weights = counts.astype(jnp.float32)
    root_weight = jnp.sqrt(weights)
    probe_rows = (probes.astype(jnp.float32) * root_weight[:, None]).astype(jnp.bfloat16)
    pheno_rows = (phenotype * root_weight).astype(jnp.bfloat16)
    count_rows = counts.astype(jnp.bfloat16)
    left_rows = jnp.stack([count_rows, pheno_rows], axis=1)
    dosage = unpack_rows(geno_words)
    cross_panel = jnp.einsum("rj,rb->jb", dosage, probe_rows, preferred_element_type=jnp.float32)
    linear = jnp.einsum("rc,rj->cj", left_rows, dosage, preferred_element_type=jnp.float32)
    squares = jnp.einsum("r,rj->j", count_rows, dosage * dosage, preferred_element_type=jnp.float32)
    moments = jnp.stack([linear[0], squares, linear[1]])
    totals = jnp.concatenate(
        [
            jnp.sum(weights)[None],
            jnp.sum(pheno_rows.astype(jnp.float32))[None],
            jnp.sum(probe_rows.astype(jnp.float32), axis=0),
        ]
    )
    levels = jnp.arange(COMPS, dtype=jnp.int32)
    member_all = (tile_comp[:, None] == levels[None, :]).astype(jnp.float32)
    comp_sizes = 128.0 * jnp.sum(member_all, axis=0)
    member_tiles = lax.dynamic_slice_in_dim(
        member_all, lax.axis_index("snp") * tile_local, tile_local, 0
    )
    member_snps = jnp.repeat(member_tiles, 128, axis=0)
    inverse = jnp.sum(member_snps * (1.0 / comp_sizes)[None, :], axis=1)
    summed_panel, summed_moments, totals = packed_total(
        (cross_panel.reshape(-1, 128), moments, totals), (("samp_0", "samp_1"), "samp_2")
    )
    average, coefficients, energy = finish(
        summed_panel.reshape(snp_local, probe_count), summed_moments, totals, inverse, member_snps
    )
    energy = of_everyone(energy, "snp")
    coef_tiles = coefficients.reshape(tile_local, 128, probe_count)
    centre = jnp.sum(average.reshape(tile_local, 128, 1) * coef_tiles.astype(jnp.float32), axis=1)
    quarter = height // lax.axis_size("snp")
    inner_count = block_number(height)
    piece_rows = height // inner_count
    dosage = unpack_rows(geno_words)
    dosage = dosage.reshape(piece_rows, tile_local, 128)
    partial_value = (
        jnp.einsum("rtj,tjb->rtb", dosage, coef_tiles, preferred_element_type=jnp.float32)
        - centre[None]
    )
    grouped = jnp.einsum(
        "rtb,tk->rkb", partial_value, member_tiles, precision=lax.Precision.HIGHEST
    )
    scaled = grouped * root_weight[:, None, None]
    pieces = scaled.reshape(piece_rows, COMPS * probe_count)
    summed_images = of_everyone(pieces, "snp")
    own_images = lax.dynamic_slice_in_dim(
        summed_images, lax.axis_index("snp") * quarter, quarter, 0
    )
    stacked = own_images.reshape(quarter, COMPS, probe_count)
    local_trace = jnp.einsum("rkb,rlb->kl", stacked, stacked, precision=lax.Precision.HIGHEST)
    trace_sum = one_axis_at_a_time(local_trace, (("samp_0", "samp_1"), ("samp_2", "snp")))
    weight_total = totals[0]
    traces = trace_sum * (SNPS / (COMPS * probe_count)) / (weight_total * weight_total)
    return (own_images.astype(jnp.bfloat16), traces, energy / weight_total)


def solution(mesh):
    split = Mesh(
        mesh.devices.reshape(16, 4, 2, mesh.shape["snp"]), ("samp_0", "samp_1", "samp_2", "snp")
    )
    return jax.shard_map(
        on_device,
        mesh=split,
        in_specs=(P(SAMP, "snp"), P(SAMP), P(SAMP, None), P(SAMP), P()),
        out_specs=(P(SAMP_SNP, None), P(), P()),
        check_vma=False,
    )
```

profile of v0, /device:TPU:1, one launch (start us, length us, event | category | flops | bytes accessed | tf_op | source)
XLA Modules:
  0.0 212.2 jit_solution(3230786590413125120)
XLA Ops:
  1.3 1.3 convert_reduce_fusion.2
  2.7 1.1 copy.65
  3.7 0.9 convert_reduce_fusion
  7.9 1.9 concatenate.3
  9.8 1.2 reshape_reshape.11
  11.1 11.1 %all_to_all.46 = f32[2,64,2145]{2,1,0:T(8,128)S(1)} all-to-all(f32[2,64,2145]{2,1,0:T(8,128)S(1)} %copy.51), channel_id=1, replica_groups=mesh['samp_0'=16,'samp_1'=4,'samp_2'=2,'snp'=4] {'samp_2'}, dimensions={0} | all-to-all | bytes 2196480 | tf_op jit(solution)/shard_map/all_to_all | solution.py:23
  22.7 45.1 %all_to_all.47 = f32[64,1,2145]{2,1,0:T(1,128)S(1)} all-to-all(f32[64,1,2145]{2,1,0:T(1,128)S(1)} %all_to_all.30), channel_id=1, replica_groups=mesh['samp_0'=16,'samp_1'=4,'samp_2'=2,'snp'=4] {'samp_0','samp_1'}, dimensions={0} | all-to-all | bytes 1098240 | tf_op jit(solution)/shard_map/all_to_all | solution.py:31
  68.2 1.2 broadcast_in_dim.24
  69.3 7.5 %all-to-all-start.2 = ((f32[64,1,2145]{2,1,0:T(1,128)}), f32[64,1,2145]{2,1,0:T(1,128)S(1)}, u32[]{:S(2)}, u32[]{:S(2)}) async-start(f32[64,1,2145]{2,1,0:T(1,128)} %broadcast_in_dim.24), calls=%async_computation.2 | async-start | bytes 1114112 | tf_op jit(solution)/shard_map/all_to_all | solution.py:42
  77.0 2.4 %shift_right_arithmetic.41 = s32[256,2,16,128]{0,3,2,1:T(8,128)} broadcast(s32[256,2,128]{0,2,1:T(8,128)S(1)} %bitcast.44), dimensions={0,1,3} | broadcast | bytes 4456448 | tf_op jit(solution)/shard_map/shift_right_arithmetic | solution.py:89
  79.5 5.6 %copy.55 = s32[256,32,128]{2,0,1:T(8,128)} copy(s32[256,32,128]{0,2,1:T(8,128)} %bitcast.39) | data formatting | bytes 8388608 | tf_op jit(solution)/shard_map/shift_right_arithmetic | solution.py:89
  85.3 21.9 %all-to-all-done.2 = f32[64,1,2145]{2,1,0:T(1,128)S(1)} async-done(((f32[64,1,2145]{2,1,0:T(1,128)}), f32[64,1,2145]{2,1,0:T(1,128)S(1)}, u32[]{:S(2)}, u32[]{:S(2)}) %all-to-all-start.2) | async-done | bytes 549152 | tf_op jit(solution)/shard_map/all_to_all | solution.py:42
  107.4 9.1 %all_to_all.48 = f32[2,64,2145]{2,1,0:T(8,128)S(1)} all-to-all(f32[2,64,2145]{2,1,0:T(8,128)S(1)} %broadcast_in_dim.26), channel_id=1, replica_groups=mesh['samp_0'=16,'samp_1'=4,'samp_2'=2,'snp'=4] {'samp_2'}, dimensions={0} | all-to-all | bytes 2196480 | tf_op jit(solution)/shard_map/all_to_all | solution.py:42
  116.4 0.9 copy.52
  117.3 0.9 reshape_reshape.12
  119.1 1.9 slice.67
  121.0 2.2 %slice.64 = f32[4290,64]{1,0:T(8,128)S(1)} reshape(f32[64,2,2145]{2,1,0:T(2,128)S(1)} %copy.52) | data formatting | bytes 2196480 | tf_op jit(solution)/shard_map/slice | solution.py:70
  123.2 1.3 fusion.28
  124.5 2.0 fusion.22
  126.5 2.5 %multiply_reduce_fusion = (f32[32,64]{1,0:T(8,128)S(1)}, bf16[4096,64]{1,0:T(8,128)(2,1)S(1)}) fusion(f32[32,128]{1,0:T(8,128)S(1)} %get-tuple-element.10, f32[4096]{0:T(1024)S(1)} %bitcast.47, f32[64]{0:T(128)S(1)} %slice.78, f32[4096]{0:T(1024)S(1)} %get-tuple-element.14, f32[4290,64]{1,0:T(8,128)S(1)} %slice.64, f32[4096]{0:T(1024)S(1)} %get-tuple-element.13), kind=kLoop, calls=%fused_computation.13 | loop fusion | flops 2357248 | bytes 1646848 | tf_op jit(solution)/shard_map/reduce_sum | solution.py:153
  129.0 3.2 %subtract_bitcast_fusion = f32[256,32,64]{0,2,1:T(8,128)S(1)} fusion(bf16[32,128,64]{2,1,0:T(8,128)(2,1)S(1)} %bitcast.42, s32[256,32,128]{2,0,1:T(8,128)} %copy.55, s32[32]{0:T(128)S(1)} %shift_right_arithmetic.49, f32[32,64]{1,0:T(8,128)S(1)} %get-tuple-element.5), kind=kOutput, calls=%fused_computation.12 | convolution fusion | flops 137887744 | bytes 6824064 | tf_op jit(solution)/shard_map/rtj,tjb->rtb/dot_general | solution.py:160
  132.2 2.0 fusion.16
  134.5 1.6 broadcast_in_dim.29
  136.2 4.0 %all-to-all-start.4 = ((f32[4,256,512]{2,1,0:T(8,128)}), f32[4,256,512]{2,1,0:T(8,128)S(1)}, u32[]{:S(2)}, u32[]{:S(2)}) async-start(f32[4,256,512]{2,1,0:T(8,128)} %broadcast_in_dim.29), calls=%async_computation.4 | async-start | bytes 4194304 | tf_op jit(solution)/shard_map/all_to_all | solution.py:42
  140.4 25.6 %all-to-all-done.4 = f32[4,256,512]{2,1,0:T(8,128)S(1)} async-done(((f32[4,256,512]{2,1,0:T(8,128)}), f32[4,256,512]{2,1,0:T(8,128)S(1)}, u32[]{:S(2)}, u32[]{:S(2)}) %all-to-all-start.4) | async-done | bytes 2097184 | tf_op jit(solution)/shard_map/all_to_all | solution.py:42
  166.6 3.2 %all-to-all-start.7 = ((f32[4,1,8]{2,1,0:T(1,128)}), f32[4,1,8]{2,1,0:T(1,128)S(1)}, u32[]{:S(2)}, u32[]{:S(2)}) async-start(f32[4,1,8]{2,1,0:T(1,128)} %broadcast_in_dim.32), calls=%async_computation.7 | async-start | bytes 4096 | tf_op jit(solution)/shard_map/all_to_all | solution.py:42
  171.5 2.4 %all-to-all-done.7 = f32[4,1,8]{2,1,0:T(1,128)S(1)} async-done(((f32[4,1,8]{2,1,0:T(1,128)}), f32[4,1,8]{2,1,0:T(1,128)S(1)}, u32[]{:S(2)}, u32[]{:S(2)}) %all-to-all-start.7) | async-done | bytes 160 | tf_op jit(solution)/shard_map/all_to_all | solution.py:42
  174.4 5.9 %all-to-all-start.5 = ((f32[8,8,8]{2,1,0:T(8,128)}), f32[8,8,8]{2,1,0:T(8,128)S(1)}, u32[]{:S(2)}, u32[]{:S(2)}) async-start(f32[8,8,8]{2,1,0:T(8,128)} %broadcast_in_dim.30), calls=%async_computation.5 | async-start | bytes 65536 | tf_op jit(solution)/shard_map/all_to_all | solution.py:42
  181.4 3.8 %all-to-all-done.5 = f32[8,8,8]{2,1,0:T(8,128)S(1)} async-done(((f32[8,8,8]{2,1,0:T(8,128)}), f32[8,8,8]{2,1,0:T(8,128)S(1)}, u32[]{:S(2)}, u32[]{:S(2)}) %all-to-all-start.5) | async-done | bytes 2080 | tf_op jit(solution)/shard_map/all_to_all | solution.py:42
  185.9 5.5 %all-to-all-start.6 = ((f32[64,8,8]{2,1,0:T(8,128)}), f32[64,8,8]{2,1,0:T(8,128)S(1)}, u32[]{:S(2)}, u32[]{:S(2)}) async-start(f32[64,8,8]{2,1,0:T(8,128)} %broadcast_in_dim.31), calls=%async_computation.6 | async-start | bytes 524288 | tf_op jit(solution)/shard_map/all_to_all | solution.py:42
  191.5 1.1 broadcast_divide_fusion
  192.6 18.9 %all-to-all-done.6 = f32[64,8,8]{2,1,0:T(8,128)S(1)} async-done(((f32[64,8,8]{2,1,0:T(8,128)}), f32[64,8,8]{2,1,0:T(8,128)S(1)}, u32[]{:S(2)}, u32[]{:S(2)}) %all-to-all-start.6) | async-done | bytes 16416 | tf_op jit(solution)/shard_map/all_to_all | solution.py:42
  (50 shorter events, 11.4 us)
Async XLA Ops:
  0.6 4.8 %copy-start.1 = (bf16[256,64]{0,1:T(8,128)(2,1)S(1)}, bf16[256,64]{0,1:T(8,128)(2,1)}, u32[]{:S(2)}) copy-start(bf16[256,64]{0,1:T(8,128)(2,1)} %param.7) | copy-start | bytes 98308
  22.3 54.5 %copy-start.2 = (s32[128]{0:T(128)S(1)}, s32[128]{0:T(128)}, u32[]{:S(2)}) copy-start(s32[128]{0:T(128)} %param.9) | copy-start | bytes 1540
  69.3 37.9 %all-to-all-start.2 = ((f32[64,1,2145]{2,1,0:T(1,128)}), f32[64,1,2145]{2,1,0:T(1,128)S(1)}, u32[]{:S(2)}, u32[]{:S(2)}) async-start(f32[64,1,2145]{2,1,0:T(1,128)} %broadcast_in_dim.24), calls=%async_computation.2 | async-start | bytes 1114112 | tf_op jit(solution)/shard_map/all_to_all | solution.py:42
  118.2 1.0 copy-start
  136.2 29.9 %all-to-all-start.4 = ((f32[4,256,512]{2,1,0:T(8,128)}), f32[4,256,512]{2,1,0:T(8,128)S(1)}, u32[]{:S(2)}, u32[]{:S(2)}) async-start(f32[4,256,512]{2,1,0:T(8,128)} %broadcast_in_dim.29), calls=%async_computation.4 | async-start | bytes 4194304 | tf_op jit(solution)/shard_map/all_to_all | solution.py:42
  166.6 7.3 %all-to-all-start.7 = ((f32[4,1,8]{2,1,0:T(1,128)}), f32[4,1,8]{2,1,0:T(1,128)S(1)}, u32[]{:S(2)}, u32[]{:S(2)}) async-start(f32[4,1,8]{2,1,0:T(1,128)} %broadcast_in_dim.32), calls=%async_computation.7 | async-start | bytes 4096 | tf_op jit(solution)/shard_map/all_to_all | solution.py:42
  174.4 10.8 %all-to-all-start.5 = ((f32[8,8,8]{2,1,0:T(8,128)}), f32[8,8,8]{2,1,0:T(8,128)S(1)}, u32[]{:S(2)}, u32[]{:S(2)}) async-start(f32[8,8,8]{2,1,0:T(8,128)} %broadcast_in_dim.30), calls=%async_computation.5 | async-start | bytes 65536 | tf_op jit(solution)/shard_map/all_to_all | solution.py:42
  185.9 25.6 %all-to-all-start.6 = ((f32[64,8,8]{2,1,0:T(8,128)}), f32[64,8,8]{2,1,0:T(8,128)S(1)}, u32[]{:S(2)}, u32[]{:S(2)}) async-start(f32[64,8,8]{2,1,0:T(8,128)} %broadcast_in_dim.31), calls=%async_computation.6 | async-start | bytes 524288 | tf_op jit(solution)/shard_map/all_to_all | solution.py:42
where the time goes:
time: 214 us; the launch traced here: 212 us
  waiting for transfers between devices  72.6 us (34%)
  blocking collectives  65.2 us (30%)
  starting transfers between devices  26.1 us (12%)
  local copies, waits for them, and re-layouts  25.5 us (12%)
  other arithmetic  13 us (6%)
  matrix products  7.76 us (4%)
    all_to_all x5, waiting for transfers between devices, sent_to_all(): lax.all_to_all(jnp.broadcast_to(shard[None], (size, *shard.shape)), axis,...  72.6 us
    all_to_all x1, blocking collectives, sum_by_axis(): lax.all_to_all(nearer, far, split_axis=0, concat_axis=0, tiled=True)  45.1 us
    all_to_all x5, starting transfers between devices, sent_to_all(): lax.all_to_all(jnp.broadcast_to(shard[None], (size, *shard.shape)), axis,...  26.1 us
    all_to_all x1, blocking collectives, sent_and_summed(): blocks = lax.all_to_all(cut_along(shard, dim, size), axis, 0, 0, tiled=True)  11.1 us
    shift_right_arithmetic x6, local copies, waits for them, and re-layouts, unpack_rows(): fields = jnp.right_shift(grouped, shifts) & 3  9.24 us
    all_to_all x1, blocking collectives, sent_to_all(): lax.all_to_all(jnp.broadcast_to(shard[None], (size, *shard.shape)), axis,...  9.05 us
    broadcast_in_dim x7, local copies, waits for them, and re-layouts, sent_to_all(): jnp.broadcast_to(shard[None], (size, *shard.shape))  4.94 us
  transfers between devices with their start and end apart: 5, of which 5 were waited for; matrix products, arithmetic and copies ran while one was open for 5% of the time, Pallas kernels for 0%

commit v1 on v0

v1 whole, which is shorter than its diff:
```python
import jax
import jax.numpy as jnp
import numpy as np
from jax import lax
from jax.experimental import pallas as pl
from jax.experimental.pallas import tpu as pltpu
from jax.sharding import Mesh
from jax.sharding import PartitionSpec as P

SNPS = 16384
COMPS = 8
PROBES = 64
EPSILON = 1e-05
F32 = jnp.float32
BF16 = jnp.bfloat16

PHENO, FIRST, SQUARE, RATE, TOTALS = 64, 65, 67, 69, 70
COUNT = 65
ROWS = 72


def rounded(v):
    return v.astype(BF16).astype(F32)


def two_parts(v):
    high = rounded(v)
    return high, v - high


def three_parts(v):
    high = rounded(v)
    rest = v - high
    mid = rounded(rest)
    return high, mid, rest - mid


def stacked(rows, height):
    width = rows[0].shape[1]
    at = lax.broadcasted_iota(jnp.int32, (height, width), 0)
    out = jnp.zeros((height, width), F32)
    for i, row in enumerate(rows):
        out = jnp.where(at == i, jnp.broadcast_to(row, (height, width)), out)
    return out


def rate_of(weight):
    return rounded(1.0 / jnp.maximum(weight, 1.0))


def dot_tn(a, b):
    return lax.dot_general(a, b, (((0,), (0,)), ((), ())), preferred_element_type=F32)


def dot_nt(a, b):
    return lax.dot_general(a, b, (((1,), (1,)), ((), ())), preferred_element_type=F32)


def dosage_tile(words, tile):
    half, field = divmod(tile, 16)
    block = words[:, 128 * half : 128 * half + 128]
    return (lax.shift_right_logical(block, jnp.int32(2 * field)) & 3).astype(F32)


def panel_kernel(words_ref, probes_ref, counts_ref, pheno_ref, out_ref):
    counts = counts_ref[...].astype(F32)
    root = jnp.sqrt(counts)
    probes = probes_ref[...].astype(F32)
    wide = jnp.concatenate([probes, jnp.zeros_like(probes)], axis=1)
    probe_rows = (wide.T[:64] * root).astype(BF16).astype(F32)
    pheno_rows = rounded(pheno_ref[...] * root)
    tail = stacked([pheno_rows, counts], 64)
    left_all = jnp.concatenate([probe_rows, tail], axis=0)
    left = left_all[:ROWS].astype(BF16)
    left_tail = left_all[64:72].astype(BF16)
    totals = dot_nt(jnp.ones((8, left_all.shape[1]), BF16), left_all.astype(BF16))[:1]
    column = jnp.sum(left_all[:ROWS], axis=1, keepdims=True)
    rate = rate_of(jnp.sum(counts, axis=1, keepdims=True))
    parts = three_parts(totals)
    totals_row = jnp.concatenate([*parts, jnp.zeros_like(totals)], axis=1)
    words = words_ref[...]
    for group in range(8):
        x = jnp.concatenate([dosage_tile(words, 4 * group + i) for i in range(4)], axis=1)
        sums = jnp.dot(left, x.astype(BF16), preferred_element_type=F32)
        squares = jnp.dot(left_tail, (x * x).astype(BF16), preferred_element_type=F32)[1:2]
        first = sums[COUNT : COUNT + 1]
        centre = rounded(first * rate)
        centred = sums - column * centre
        lower = stacked(
            [
                centred[PHENO : PHENO + 1],
                *two_parts(first),
                *two_parts(squares),
                jnp.broadcast_to(rate, first.shape),
                totals_row,
            ],
            8,
        )
        out_ref[group] = jnp.concatenate([centred[:64], lower], axis=0).astype(BF16)


def lane_group(shape):
    return lax.broadcasted_iota(jnp.int32, shape, 1) // 32


def regroup_kernel(in_ref, out_ref):
    total = jnp.zeros((ROWS, 512), F32)
    centres, parts = [], [[], [], []]
    for d in range(8):
        block = in_ref[d].astype(F32)
        total = total + block
        first = block[FIRST : FIRST + 1] + block[FIRST + 1 : FIRST + 2]
        centres.append(first * block[RATE : RATE + 1])
        for s in range(3):
            parts[s].append(block[TOTALS : TOTALS + 1, 128 * s : 128 * s + 128])
    centre8 = stacked(centres, 8)
    left = jnp.concatenate([stacked(rows, 8) for rows in parts], axis=0)
    totals = jnp.sum(left, axis=0, keepdims=True)
    lane = lax.broadcasted_iota(jnp.int32, totals.shape, 1)
    weight = jnp.sum(jnp.where(lane == COUNT, totals, 0.0), axis=1, keepdims=True)
    rate = rate_of(weight)
    first = total[FIRST : FIRST + 1] + total[FIRST + 1 : FIRST + 2]
    squares = total[SQUARE : SQUARE + 1] + total[SQUARE + 1 : SQUARE + 2]
    centre = jnp.broadcast_to(first * rate, (8, 512))
    right = jnp.concatenate([centre8] * 3 + [centre] * 3, axis=0).astype(BF16)
    left = jnp.concatenate([left, -left], axis=0).astype(BF16)
    centred = total + dot_tn(left, right)[:ROWS]
    lower = stacked(
        [
            centred[PHENO : PHENO + 1],
            *two_parts(first),
            *two_parts(squares),
            jnp.broadcast_to(rate, first.shape),
        ],
        8,
    )
    full = jnp.concatenate([centred[:64], lower], axis=0)
    rows = []
    for part in three_parts(totals):
        for k in range(3):
            rows.append(pltpu.roll(part, (96 - 24 * k) % 128, 1) if 96 - 24 * k else part)
    totals_block = stacked(rows, 24)
    group = lane_group((24, 128))
    for tile in range(4):
        blocks = [full[24 * k : 24 * k + 24, 128 * tile : 128 * tile + 128] for k in range(3)]
        for q in range(4):
            packed = totals_block
            for k in range(3):
                shift = (32 * (k - q)) % 128
                moved = pltpu.roll(blocks[k], shift, 1) if shift else blocks[k]
                packed = jnp.where(group == k, moved, packed)
            out_ref[4 * tile + q] = packed.astype(BF16)


def finish_kernel(place_ref, comp_ref, in_ref, coef_ref, extra_ref):
    total = jnp.zeros((24, 128), F32)
    group16 = lane_group((16, 128))
    lane16 = lax.broadcasted_iota(jnp.int32, (16, 128), 1)
    centres, parts = [], [[] for _ in range(9)]
    for d in range(16):
        block = in_ref[d].astype(F32)
        total = total + block
        first = block[FIRST - 48 : FIRST - 47] + block[FIRST - 47 : FIRST - 46]
        centres.append(first * block[RATE - 48 : RATE - 47])
        for i in range(9):
            parts[i].append(block[i : i + 1])
    centre16 = jnp.where(group16 == 2, rounded(stacked(centres, 16)), 0.0)
    kept = (lane16 >= 96) & (lane16 < 120)
    left = jnp.concatenate([jnp.where(kept, stacked(rows, 16), 0.0) for rows in parts], axis=0)
    moved = [pltpu.roll(centre16, 64, 1), pltpu.roll(centre16, 96, 1), centre16]
    marks = [(group16 == k).astype(F32) for k in range(3)]
    right = jnp.concatenate(
        [jnp.concatenate(moved * 3, axis=0), jnp.concatenate(marks * 3, axis=0)], axis=1
    )
    outer = dot_tn(left.astype(BF16), right.astype(BF16))[96:120]
    cross = total + outer[:, :128]
    column_totals = outer[:, 128:]
    group1 = lane_group((1, 128))
    here = group1 == 2
    weight = column_totals[COUNT - 48 : COUNT - 47]
    weight = jnp.where(here, weight, 1.0)
    first = total[FIRST - 48 : FIRST - 47] + total[FIRST - 47 : FIRST - 46]
    squares = total[SQUARE - 48 : SQUARE - 47] + total[SQUARE - 47 : SQUARE - 46]
    average = jnp.where(here, first / weight, 0.0)
    second = jnp.where(here, squares / weight, 0.0)
    spread = jnp.where(here, 1.0 / jnp.sqrt(second - average * average + EPSILON), 0.0)

    def everywhere(row):
        return row + pltpu.roll(row, 64, 1) + pltpu.roll(row, 96, 1)

    spread_all = everywhere(spread)
    unit = spread_all * (cross - everywhere(average) * column_totals)
    lane1 = lax.broadcasted_iota(jnp.int32, (1, 128), 1)
    comps = comp_ref[...]
    comp = jnp.sum(jnp.where(lane1 == place_ref[0], comps, 0), axis=1, keepdims=True)
    size = 128.0 * jnp.sum((comps == comp).astype(F32), axis=1, keepdims=True)
    inverse = 1.0 / size
    coefficients = spread_all * unit * inverse
    pheno_unit = jnp.where(here, unit[PHENO - 48 : PHENO - 47], 0.0)
    energy = jnp.sum(pheno_unit * pheno_unit * inverse, axis=1, keepdims=True)
    parts = three_parts(average)
    row = lax.broadcasted_iota(jnp.int32, (24, 128), 0)
    group = lane_group((24, 128))
    last = jnp.where(row < 16, coefficients, stacked([average] * 16 + list(parts), 24))
    packed = jnp.where(group == 2, last, jnp.where(group < 2, coefficients, 0.0)).astype(BF16)
    for d in range(16):
        coef_ref[d] = packed
    weight_all = jnp.sum(jnp.where(lane1 == 64, weight, 0.0), axis=1, keepdims=True)
    extra_ref[...] = stacked(
        [
            jnp.where(lane1 == 64 + comp, energy, 0.0),
            jnp.broadcast_to(weight_all, (1, 128)),
        ],
        8,
    )


def images_kernel(place_ref, comp_ref, words_ref, counts_ref, coef_ref, out_ref, acc_ref):
    acc_ref[...] = jnp.zeros_like(acc_ref)
    words = words_ref[...]
    group = lane_group((24, 128))
    first_tile = place_ref[1]
    for tile in range(32):
        blocks = [coef_ref[tile // 4, 4 * (tile % 4) + q].astype(F32) for q in range(4)]
        rows = []
        for k in range(3):
            row = None
            for q in range(4):
                shift = (32 * (q - k)) % 128
                moved = pltpu.roll(blocks[q], shift, 1) if shift else blocks[q]
                row = moved if row is None else jnp.where(group == q, moved, row)
            rows.append(row)
        weights = jnp.concatenate(rows, axis=0)
        x = jnp.concatenate([dosage_tile(words, tile), weights[64:72]], axis=0).astype(BF16)
        product = dot_nt(x, weights[:64].astype(BF16))
        comp = comp_ref[first_tile + tile]
        acc_ref[comp] = acc_ref[comp] + product
    root = jnp.sqrt(counts_ref[...].astype(F32))
    column = jnp.broadcast_to(root, (128, root.shape[1])).T
    for pair in range(4):
        halves = []
        for k in (2 * pair, 2 * pair + 1):
            total = acc_ref[k]
            centre = total[256:257] + total[257:258] + total[258:259]
            halves.append(total[:256] - centre)
        out_ref[:, 128 * pair : 128 * pair + 128] = (
            jnp.concatenate(halves, axis=1) * column
        ).astype(BF16)


def trace_places():
    low, high = np.zeros((24, 128), np.float32), np.zeros((24, 128), np.float32)
    r = 0
    for turned in (0, 1):
        for a in range(4):
            for b in range(a, 4):
                for table, k, l in (
                    (low, 2 * a, 2 * b + turned),
                    (high, 2 * a + 1, 2 * b + 1 - turned),
                ):
                    if turned and a == b and table is high:
                        continue
                    table[r, 8 * k + l] = 1.0
                    table[r, 8 * l + k] = 1.0
                r += 1
    return low, high


def trace_kernel(in_ref, extra_ref, low_ref, high_ref, images_ref, sums_ref):
    full = in_ref[0].astype(F32)
    for d in range(1, 4):
        full = full + in_ref[d].astype(F32)
    images_ref[...] = full.astype(BF16)
    tiles = [full[:, 128 * a : 128 * a + 128] for a in range(4)]
    turned = [pltpu.roll(t, 64, 1) for t in tiles]
    rows = []
    for others in (tiles, turned):
        for a in range(4):
            for b in range(a, 4):
                rows.append(jnp.sum(tiles[a] * others[b], axis=0, keepdims=True))
    products = stacked(rows, 24)
    lane = lax.broadcasted_iota(jnp.int32, products.shape, 1)
    low = jnp.sum(jnp.where(lane < 64, products, 0.0), axis=1, keepdims=True)
    high = jnp.sum(jnp.where(lane < 64, 0.0, products), axis=1, keepdims=True)
    sums = jnp.sum(low * low_ref[...] + high * high_ref[...], axis=0, keepdims=True)
    sums = sums + extra_ref[0:1]
    sums_ref[...] = jnp.broadcast_to(sums[None], sums_ref.shape)


def call(kernel, out, scalars=0, **kwargs):
    def run(*args):
        specs = [pl.BlockSpec(memory_space=pltpu.SMEM)] * scalars
        specs += [pl.BlockSpec(memory_space=pltpu.VMEM)] * (len(args) - scalars)
        return pl.pallas_call(kernel, out_shape=out, in_specs=specs, **kwargs)(*args)

    return run


def shape(dims, dtype):
    return jax.ShapeDtypeStruct(dims, dtype)


def on_device(geno_words, counts, probes, phenotype, tile_comp):
    y, c, x = lax.axis_index("y"), lax.axis_index("c"), lax.axis_index("x")
    z = lax.axis_index("z")
    first_tile = 32 * x
    place = jnp.stack([first_tile + 4 * (2 * y + c) + z // 4, first_tile]).astype(jnp.int32)
    counts_row = counts.reshape(1, -1)
    comp_row = tile_comp.reshape(1, -1)
    sent = call(panel_kernel, shape((8, ROWS, 512), BF16))(
        geno_words, probes, counts_row, phenotype.reshape(1, -1)
    )
    got = lax.all_to_all(sent, ("y", "c"), 0, 0, tiled=True)
    sent = call(regroup_kernel, shape((16, 24, 128), BF16))(got)
    got = lax.all_to_all(sent, "z", 0, 0, tiled=True)
    sent, extra = call(
        finish_kernel, (shape((16, 24, 128), BF16), shape((8, 128), F32)), scalars=1
    )(place, comp_row, got)
    got = lax.all_to_all(sent, "z", 0, 0, tiled=True)
    coefficients = lax.all_gather(got, ("y", "c"))
    partial = call(
        images_kernel,
        shape((256, COMPS * PROBES), BF16),
        scalars=2,
        scratch_shapes=[pltpu.VMEM((COMPS, 264, PROBES), F32)],
    )(place, tile_comp, geno_words, counts_row, coefficients)
    pieces = lax.all_to_all(partial.reshape(4, 64, COMPS * PROBES), "x", 0, 0, tiled=True)
    low, high = trace_places()
    images, sums = call(
        trace_kernel, (shape((64, COMPS * PROBES), BF16), shape((16, 1, 128), F32))
    )(pieces, extra, jnp.asarray(low), jnp.asarray(high))
    sums = jnp.sum(lax.all_to_all(sums, "z", 0, 0, tiled=True), axis=0)
    sums = jnp.broadcast_to(sums[None], (32, 1, 128))
    sums = jnp.sum(lax.all_to_all(sums, ("y", "c", "x"), 0, 0, tiled=True), axis=0)[0]
    weight_total = extra[1, 0]
    traces = sums[:64].reshape(8, 8) * (SNPS / (COMPS * PROBES)) / (weight_total * weight_total)
    return images, traces, sums[64:72] / weight_total


def solution(mesh):
    split = Mesh(mesh.devices.reshape(16, 4, 2, 4), ("z", "y", "c", "x"))
    samples = ("z", "y", "c")
    return jax.shard_map(
        on_device,
        mesh=split,
        in_specs=(P(samples, "x"), P(samples), P(samples, None), P(samples), P()),
        out_specs=(P((*samples, "x"), None), P(), P()),
        check_vma=False,
    )
```

time: 214 us -> 134 us (0.63)
  waiting for transfers between devices: 72.6 us -> 16 us
  local copies, waits for them, and re-layouts: 25.5 us -> 4.59 us
  blocking collectives: 65.2 us -> 80.5 us
  Pallas kernels: 0 us -> 12.2 us
  other arithmetic: 13 us -> 1.8 us
  starting transfers between devices: 26.1 us -> 15.9 us
  matrix products: 7.76 us -> 0 us
    all_to_all x5 -> x2, waiting for transfers between devices: 72.6 us -> 16 us  [the longest x1 11.2 us: on_device(): got = lax.all_to_all(sent, 'z', 0, 0, tiled=True)]
    all_gather x0 -> x1, blocking collectives: none -> 17.4 us  [on_device(): coefficients = lax.all_gather(got, ('y', 'c'))]
    pallas_call x0 -> x5, Pallas kernels: none -> 12.2 us  [run(): pl.pallas_call(kernel, out_shape=out, in_specs=specs, **kwargs)(*args)]
    all_to_all x5 -> x2, starting transfers between devices: 26.1 us -> 15.9 us  [the longest x1 9.97 us: on_device(): got = lax.all_to_all(sent, 'z', 0, 0, tiled=True)]
    shift_right_arithmetic x6 -> x0, local copies, waits for them, and re-layouts: 9.24 us -> none  [unpack_rows(): fields = jnp.right_shift(grouped, shifts) & 3]
    dot_general x6 -> x0, matrix products: 7.76 us -> none  [the longest x1 3.15 us: on_device(): jnp.einsum('rtj,tjb->rtb', dosage, coef_tiles, preferred_element_type=jnp...]
    reduce_sum x12 -> x2, other arithmetic: 5.94 us -> 0.05 us  [the longest x1 0.03 us: on_device(): sums = jnp.sum(lax.all_to_all(sums, 'z', 0, 0, tiled=True), axis=0)]
    broadcast_in_dim x7 -> x1, local copies, waits for them, and re-layouts: 4.94 us -> 0.61 us  [on_device(): sums = jnp.broadcast_to(sums[None], (32, 1, 128))]
  transfers between devices with their start and end apart: 5 -> 2, of which waited for: 5 -> 2; matrix products, arithmetic and copies ran while one was open for 5% -> 1% of each run, Pallas kernels for 0% -> 0%
where the time goes in v1:
time: 134 us; the launch traced here: 133 us
  blocking collectives  80.5 us (60%)
  waiting for transfers between devices  16 us (12%)
  starting transfers between devices  15.9 us (12%)
  Pallas kernels  12.2 us (9%)
  local copies, waits for them, and re-layouts  4.59 us (3%)
  other arithmetic  1.8 us (1%)
  between operations  1.8 us (1%)
    all_to_all x1, blocking collectives, on_device(): got = lax.all_to_all(sent, ('y', 'c'), 0, 0, tiled=True)  21.3 us
    all_gather x1, blocking collectives, on_device(): coefficients = lax.all_gather(got, ('y', 'c'))  17.4 us
    all_to_all x1, blocking collectives, on_device(): got = lax.all_to_all(sent, 'z', 0, 0, tiled=True)  16.6 us
    all_to_all x1, blocking collectives, on_device(): sums = jnp.sum(lax.all_to_all(sums, 'z', 0, 0, tiled=True), axis=0)  14.7 us
    pallas_call x5, Pallas kernels, run(): pl.pallas_call(kernel, out_shape=out, in_specs=specs, **kwargs)(*args)  12.2 us
    all_to_all x1, waiting for transfers between devices, on_device(): got = lax.all_to_all(sent, 'z', 0, 0, tiled=True)  11.2 us
    all_to_all x1, blocking collectives, on_device(): lax.all_to_all(partial.reshape(4, 64, COMPS * PROBES), 'x', 0, 0, tiled=T...  10.4 us
    all_to_all x1, starting transfers between devices, on_device(): got = lax.all_to_all(sent, 'z', 0, 0, tiled=True)  9.97 us
  transfers between devices with their start and end apart: 2, of which 2 were waited for; matrix products, arithmetic and copies ran while one was open for 1% of the time, Pallas kernels for 0%

profile of v1, /device:TPU:1, one launch (start us, length us, event | category | flops | bytes accessed | tf_op | source)
XLA Modules:
  0.0 132.8 jit_solution(8419280302786726144)
XLA Ops:
  0.6 1.5 %copy.13.probes_ref = bf16[256,64]{1,0:T(8,128)(2,1)} copy(bf16[256,64]{0,1:T(8,128)(2,1)} %param.9) | data formatting | bytes 65536 | tf_op args[2]
  2.1 2.8 %shard_map.94 = bf16[8,72,512]{2,1,0:T(8,128)(2,1)} custom-call(s32[256,256]{1,0:T(8,128)} %words_ref.3, bf16[256,64]{1,0:T(8,128)(2,1)} %copy.13.probes_ref, s32[1,256]{1,0:T(1,128)} %bitcast.15, f32[1,256]{1,0:T(1,128)} %bitcast.18), custom_call_target="tpu_custom_call" | custom-call | tf_op jit(solution)/shard_map/pallas_call | solution.py:294
  5.0 21.3 %all_to_all.30.in_ref = bf16[8,72,512]{2,1,0:T(8,128)(2,1)} all-to-all(bf16[8,72,512]{2,1,0:T(8,128)(2,1)} %shard_map.94), channel_id=1, replica_groups=mesh['z'=16,'y'=4,'c'=2,'x'=4] {'y','c'}, dimensions={0} | all-to-all | bytes 1179648 | tf_op jit(solution)/shard_map/all_to_all | solution.py:313
  26.3 2.1 %shard_map.95 = bf16[16,24,128]{2,1,0:T(8,128)(2,1)} custom-call(bf16[8,72,512]{2,1,0:T(8,128)(2,1)} %all_to_all.30.in_ref), custom_call_target="tpu_custom_call" | custom-call | tf_op jit(solution)/shard_map/pallas_call | solution.py:294
  28.4 10.0 %all-to-all-start.1 = ((bf16[16,24,128]{2,1,0:T(8,128)(2,1)}), bf16[16,24,128]{2,1,0:T(8,128)(2,1)S(1)}, u32[]{:S(2)}, u32[]{:S(2)}) async-start(bf16[16,24,128]{2,1,0:T(8,128)(2,1)} %shard_map.95), calls=%async_computation.1 | async-start | bytes 196608 | tf_op jit(solution)/shard_map/all_to_all | solution.py:315
  38.4 0.6 pad_add_fusion.place_ref
  38.9 11.2 %all-to-all-done.1.in_ref = bf16[16,24,128]{2,1,0:T(8,128)(2,1)S(1)} async-done(((bf16[16,24,128]{2,1,0:T(8,128)(2,1)}), bf16[16,24,128]{2,1,0:T(8,128)(2,1)S(1)}, u32[]{:S(2)}, u32[]{:S(2)}) %all-to-all-start.1) | async-done | bytes 98336 | tf_op jit(solution)/shard_map/all_to_all | solution.py:315
  50.2 0.0 copy-start
  50.2 0.6 copy-done
  50.8 2.0 %shard_map.96 = (bf16[16,24,128]{2,1,0:T(8,128)(2,1)}, f32[8,128]{1,0:T(8,128)}) custom-call(s32[2]{0:T(128)} %pad_add_fusion.place_ref, s32[1,128]{1,0:T(1,128)} %bitcast.17, bf16[16,24,128]{2,1,0:T(8,128)(2,1)} %copy-done), custom_call_target="tpu_custom_call" | custom-call | tf_op jit(solution)/shard_map/pallas_call | solution.py:294
  52.8 16.6 %all_to_all.31 = bf16[16,24,128]{2,1,0:T(8,128)(2,1)S(1)} all-to-all(bf16[16,24,128]{2,1,0:T(8,128)(2,1)} %get-tuple-element.7), channel_id=1, replica_groups=mesh['z'=16,'y'=4,'c'=2,'x'=4] {'z'}, dimensions={0} | all-to-all | bytes 196608 | tf_op jit(solution)/shard_map/all_to_all | solution.py:319
  69.4 17.4 %all-gather = bf16[128,24,128]{2,1,0:T(8,128)(2,1)} all-gather(bf16[16,24,128]{2,1,0:T(8,128)(2,1)S(1)} %all_to_all.31), channel_id=2, replica_groups=mesh['z'=16,'y'=4,'c'=2,'x'=4] {'y','c'}, dimensions={0}, use_global_device_ids=true | all-gather | bytes 884736 | tf_op jit(solution)/shard_map/all_gather | solution.py:320
  86.8 3.6 %shard_map.97 = bf16[256,512]{1,0:T(8,128)(2,1)} custom-call(s32[2]{0:T(128)} %pad_add_fusion.place_ref, s32[128]{0:T(128)} %comp_ref.1, s32[256,256]{1,0:T(8,128)} %words_ref.3, s32[1,256]{1,0:T(1,128)} %bitcast.16, bf16[8,16,24,128]{3,2,1,0:T(8,128)(2,1)} %bitcast.12), custom_call_target="tpu_custom_call" | custom-call | tf_op jit(solution)/shard_map/pallas_call | solution.py:294
  90.4 10.4 %all_to_all.32.in_ref = bf16[4,64,512]{2,1,0:T(8,128)(2,1)} all-to-all(bf16[4,64,512]{2,1,0:T(8,128)(2,1)} %bitcast.13), channel_id=1, replica_groups=mesh['z'=16,'y'=4,'c'=2,'x'=4] {'x'}, dimensions={0} | all-to-all | bytes 524288 | tf_op jit(solution)/shard_map/all_to_all | solution.py:327
  100.8 1.8 %shard_map.98 = (bf16[64,512]{1,0:T(8,128)(2,1)}, f32[16,1,128]{2,1,0:T(1,128)}) custom-call(bf16[4,64,512]{2,1,0:T(8,128)(2,1)} %all_to_all.32.in_ref, f32[8,128]{1,0:T(8,128)} %get-tuple-element.8.extra_ref, f32[24,128]{1,0:T(8,128)} %constant.46.clone.low_ref, f32[24,128]{1,0:T(8,128)} %constant.47.clone.high_ref), custom_call_target="tpu_custom_call" | custom-call | tf_op jit(solution)/shard_map/pallas_call | solution.py:294
  102.6 14.7 %all_to_all.33 = f32[16,1,128]{2,1,0:T(1,128)S(1)} all-to-all(f32[16,1,128]{2,1,0:T(1,128)} %get-tuple-element.10), channel_id=1, replica_groups=mesh['z'=16,'y'=4,'c'=2,'x'=4] {'z'}, dimensions={0} | all-to-all | bytes 16384 | tf_op jit(solution)/shard_map/all_to_all | solution.py:332
  117.3 0.6 broadcast_in_dim.2
  117.9 5.9 %all-to-all-start.5 = ((f32[32,1,128]{2,1,0:T(1,128)}), f32[32,1,128]{2,1,0:T(1,128)S(1)}, u32[]{:S(2)}, u32[]{:S(2)}) async-start(f32[32,1,128]{2,1,0:T(1,128)} %broadcast_in_dim.2), calls=%async_computation.5 | async-start | bytes 32768 | tf_op jit(solution)/shard_map/all_to_all | solution.py:334
  123.9 1.2 slice.12
  126.2 4.7 %all-to-all-done.5 = f32[32,1,128]{2,1,0:T(1,128)S(1)} async-done(((f32[32,1,128]{2,1,0:T(1,128)}), f32[32,1,128]{2,1,0:T(1,128)S(1)}, u32[]{:S(2)}, u32[]{:S(2)}) %all-to-all-start.5) | async-done | bytes 16416 | tf_op jit(solution)/shard_map/all_to_all | solution.py:334
  130.9 1.1 divide_bitcast_fusion
  132.1 0.7 div.31
  (3 shorter events, 0.1 us)
Async XLA Ops:
  28.4 21.8 %all-to-all-start.1 = ((bf16[16,24,128]{2,1,0:T(8,128)(2,1)}), bf16[16,24,128]{2,1,0:T(8,128)(2,1)S(1)}, u32[]{:S(2)}, u32[]{:S(2)}) async-start(bf16[16,24,128]{2,1,0:T(8,128)(2,1)} %shard_map.95), calls=%async_computation.1 | async-start | bytes 196608 | tf_op jit(solution)/shard_map/all_to_all | solution.py:315
  50.2 0.6 copy-start
  117.9 13.0 %all-to-all-start.5 = ((f32[32,1,128]{2,1,0:T(1,128)}), f32[32,1,128]{2,1,0:T(1,128)S(1)}, u32[]{:S(2)}, u32[]{:S(2)}) async-start(f32[32,1,128]{2,1,0:T(1,128)} %broadcast_in_dim.2), calls=%async_computation.5 | async-start | bytes 32768 | tf_op jit(solution)/shard_map/all_to_all | solution.py:334

commit v2 on v1

--- a/solution.py
+++ b/solution.py
@@ -65,9 +65,7 @@
 def panel_kernel(words_ref, probes_ref, counts_ref, pheno_ref, out_ref):
     counts = counts_ref[...].astype(F32)
     root = jnp.sqrt(counts)
-    probes = probes_ref[...].astype(F32)
-    wide = jnp.concatenate([probes, jnp.zeros_like(probes)], axis=1)
-    probe_rows = (wide.T[:64] * root).astype(BF16).astype(F32)
+    probe_rows = rounded(probes_ref[...].astype(F32) * root)
     pheno_rows = rounded(pheno_ref[...] * root)
     tail = stacked([pheno_rows, counts], 64)
     left_all = jnp.concatenate([probe_rows, tail], axis=0)
@@ -152,7 +150,7 @@
             out_ref[4 * tile + q] = packed.astype(BF16)
 
 
-def finish_kernel(place_ref, comp_ref, in_ref, coef_ref, extra_ref):
+def finish_kernel(comp_ref, in_ref, coef_ref, extra_ref):
     total = jnp.zeros((24, 128), F32)
     group16 = lane_group((16, 128))
     lane16 = lax.broadcasted_iota(jnp.int32, (16, 128), 1)
@@ -191,8 +189,10 @@
     spread_all = everywhere(spread)
     unit = spread_all * (cross - everywhere(average) * column_totals)
     lane1 = lax.broadcasted_iota(jnp.int32, (1, 128), 1)
+    z, y, c, x = (lax.axis_index(name) for name in "zycx")
+    tile = 32 * x + 8 * y + 4 * c + lax.shift_right_logical(z, 2)
     comps = comp_ref[...]
-    comp = jnp.sum(jnp.where(lane1 == place_ref[0], comps, 0), axis=1, keepdims=True)
+    comp = jnp.sum(jnp.where(lane1 == tile, comps, 0), axis=1, keepdims=True)
     size = 128.0 * jnp.sum((comps == comp).astype(F32), axis=1, keepdims=True)
     inverse = 1.0 / size
     coefficients = spread_all * unit * inverse
@@ -215,13 +215,10 @@
     )
 
 
-def images_kernel(place_ref, comp_ref, words_ref, counts_ref, coef_ref, out_ref, acc_ref):
-    acc_ref[...] = jnp.zeros_like(acc_ref)
-    words = words_ref[...]
+def unpack_kernel(in_ref, out_ref):
     group = lane_group((24, 128))
-    first_tile = place_ref[1]
-    for tile in range(32):
-        blocks = [coef_ref[tile // 4, 4 * (tile % 4) + q].astype(F32) for q in range(4)]
+    for tile in range(4):
+        blocks = [in_ref[4 * tile + q].astype(F32) for q in range(4)]
         rows = []
         for k in range(3):
             row = None
@@ -230,7 +227,19 @@
                 moved = pltpu.roll(blocks[q], shift, 1) if shift else blocks[q]
                 row = moved if row is None else jnp.where(group == q, moved, row)
             rows.append(row)
-        weights = jnp.concatenate(rows, axis=0)
+        whole = jnp.concatenate(rows, axis=0).astype(BF16)
+        for d in range(4):
+            out_ref[d, :, 128 * tile : 128 * tile + 128] = whole
+
+
+def images_kernel(comp_ref, words_ref, counts_ref, coef_ref, out_ref, acc_ref):
+    acc_ref[...] = jnp.zeros_like(acc_ref)
+    words = words_ref[...]
+    first_tile = 32 * lax.axis_index("x")
+    for tile in range(32):
+        y, c = divmod(tile // 4, 2)
+        at = 128 * (tile % 4)
+        weights = coef_ref[c, y, :, at : at + 128].astype(F32)
         x = jnp.concatenate([dosage_tile(words, tile), weights[64:72]], axis=0).astype(BF16)
         product = dot_nt(x, weights[:64].astype(BF16))
         comp = comp_ref[first_tile + tile]
@@ -287,6 +296,19 @@
     sums_ref[...] = jnp.broadcast_to(sums[None], sums_ref.shape)
 
 
+def middle_kernel(in_ref, out_ref):
+    out_ref[...] = jnp.broadcast_to(jnp.sum(in_ref[...], axis=0, keepdims=True), out_ref.shape)
+
+
+def last_kernel(in_ref, extra_ref, traces_ref, yky_ref):
+    sums = jnp.sum(in_ref[...], axis=0)
+    weight = extra_ref[1:2]
+    scaled = sums * (SNPS / (COMPS * PROBES)) / (weight * weight)
+    rows = [scaled] + [pltpu.roll(scaled, 128 - 8 * k, 1) for k in range(1, 8)]
+    traces_ref[...] = stacked(rows, 8)[:, :8]
+    yky_ref[...] = pltpu.roll(sums / weight, 64, 1)[:, :8]
+
+
 def call(kernel, out, scalars=0, **kwargs):
     def run(*args):
         specs = [pl.BlockSpec(memory_space=pltpu.SMEM)] * scalars
@@ -296,45 +318,48 @@
     return run
 
 
+def near(array):
+    return pltpu.with_memory_space_constraint(array, pltpu.VMEM)
+
+
 def shape(dims, dtype):
     return jax.ShapeDtypeStruct(dims, dtype)
 
 
 def on_device(geno_words, counts, probes, phenotype, tile_comp):
-    y, c, x = lax.axis_index("y"), lax.axis_index("c"), lax.axis_index("x")
-    z = lax.axis_index("z")
-    first_tile = 32 * x
-    place = jnp.stack([first_tile + 4 * (2 * y + c) + z // 4, first_tile]).astype(jnp.int32)
     counts_row = counts.reshape(1, -1)
     comp_row = tile_comp.reshape(1, -1)
-    sent = call(panel_kernel, shape((8, ROWS, 512), BF16))(
-        geno_words, probes, counts_row, phenotype.reshape(1, -1)
+    sent = call(panel_kernel, pltpu.VMEM((8, ROWS, 512), BF16))(
+        geno_words, probes.T, counts_row, phenotype.reshape(1, -1)
     )
     got = lax.all_to_all(sent, ("y", "c"), 0, 0, tiled=True)
-    sent = call(regroup_kernel, shape((16, 24, 128), BF16))(got)
+    sent = call(regroup_kernel, pltpu.VMEM((16, 24, 128), BF16))(near(got))
     got = lax.all_to_all(sent, "z", 0, 0, tiled=True)
     sent, extra = call(
-        finish_kernel, (shape((16, 24, 128), BF16), shape((8, 128), F32)), scalars=1
-    )(place, comp_row, got)
+        finish_kernel, (pltpu.VMEM((16, 24, 128), BF16), pltpu.VMEM((8, 128), F32))
+    )(comp_row, near(got))
     got = lax.all_to_all(sent, "z", 0, 0, tiled=True)
-    coefficients = lax.all_gather(got, ("y", "c"))
+    sent = call(unpack_kernel, pltpu.VMEM((4, ROWS, 512), BF16))(near(got))
+    got = lax.all_to_all(sent, "y", 0, 0, tiled=True)
+    coefficients = lax.all_gather(got, "c")
     partial = call(
         images_kernel,
-        shape((256, COMPS * PROBES), BF16),
-        scalars=2,
+        pltpu.VMEM((256, COMPS * PROBES), BF16),
+        scalars=1,
         scratch_shapes=[pltpu.VMEM((COMPS, 264, PROBES), F32)],
-    )(place, tile_comp, geno_words, counts_row, coefficients)
+    )(tile_comp, geno_words, counts_row, near(coefficients))
     pieces = lax.all_to_all(partial.reshape(4, 64, COMPS * PROBES), "x", 0, 0, tiled=True)
     low, high = trace_places()
     images, sums = call(
-        trace_kernel, (shape((64, COMPS * PROBES), BF16), shape((16, 1, 128), F32))
-    )(pieces, extra, jnp.asarray(low), jnp.asarray(high))
-    sums = jnp.sum(lax.all_to_all(sums, "z", 0, 0, tiled=True), axis=0)
-    sums = jnp.broadcast_to(sums[None], (32, 1, 128))
-    sums = jnp.sum(lax.all_to_all(sums, ("y", "c", "x"), 0, 0, tiled=True), axis=0)[0]
-    weight_total = extra[1, 0]
-    traces = sums[:64].reshape(8, 8) * (SNPS / (COMPS * PROBES)) / (weight_total * weight_total)
-    return images, traces, sums[64:72] / weight_total
+        trace_kernel, (shape((64, COMPS * PROBES), BF16), pltpu.VMEM((16, 1, 128), F32))
+    )(near(pieces), near(extra), jnp.asarray(low), jnp.asarray(high))
+    got = lax.all_to_all(sums, "z", 0, 0, tiled=True)
+    sums = call(middle_kernel, pltpu.VMEM((32, 1, 128), F32))(near(got))
+    got = lax.all_to_all(sums, ("y", "c", "x"), 0, 0, tiled=True)
+    traces, yky = call(last_kernel, (shape((8, 8), F32), shape((1, 8), F32)))(
+        near(got), near(extra)
+    )
+    return images, traces, yky.reshape(8)
 
 
 def solution(mesh):

time: 134 us -> 119 us (0.89)
  blocking collectives: 80.5 us -> 110 us
  waiting for transfers between devices: 16 us -> 0 us
  starting transfers between devices: 15.9 us -> 0 us
  local copies, waits for them, and re-layouts: 4.59 us -> 0 us
  Pallas kernels: 12.2 us -> 8.21 us
  other arithmetic: 1.8 us -> 0 us
    all_to_all x1 -> x2, blocking collectives: 16.6 us -> 39.5 us  [on_device(): got = lax.all_to_all(sent, 'z', 0, 0, tiled=True)]
    all_to_all x1 -> x3, blocking collectives: 14.7 us -> 35.2 us  [the longest x1 13.9 us: on_device(): got = lax.all_to_all(sums, 'z', 0, 0, tiled=True)]
    all_to_all x2 -> x0, waiting for transfers between devices: 16 us -> none  [the longest x1 11.2 us: on_device(): got = lax.all_to_all(sent, 'z', 0, 0, tiled=True)]
    all_to_all x2 -> x0, starting transfers between devices: 15.9 us -> none  [the longest x1 9.97 us: on_device(): got = lax.all_to_all(sent, 'z', 0, 0, tiled=True)]
    all_gather x1, blocking collectives: 17.4 us -> 6.07 us  [on_device(): coefficients = lax.all_gather(got, 'c')]
    pallas_call x5 -> x8, Pallas kernels: 12.2 us -> 8.21 us  [run(): pl.pallas_call(kernel, out_shape=out, in_specs=specs, **kwargs)(*args)]
    unnamed x3 -> x0, local copies, waits for them, and re-layouts: 2.11 us -> none
    all_to_all x1, blocking collectives: 21.3 us -> 19.5 us  [on_device(): got = lax.all_to_all(sent, ('y', 'c'), 0, 0, tiled=True)]
  transfers between devices with their start and end apart: 2 -> 0, of which waited for: 2 -> 0; matrix products, arithmetic and copies ran while one was open for 1% -> 0% of each run, Pallas kernels for 0% -> 0%
where the time goes in v2:
time: 119 us
  blocking collectives  110 us (92%)
  Pallas kernels  8.21 us (7%)
    all_to_all x2, blocking collectives, on_device(): got = lax.all_to_all(sent, 'z', 0, 0, tiled=True)  39.5 us
    all_to_all x1, blocking collectives, on_device(): got = lax.all_to_all(sent, ('y', 'c'), 0, 0, tiled=True)  19.5 us
    all_to_all x1, blocking collectives, on_device(): got = lax.all_to_all(sums, 'z', 0, 0, tiled=True)  13.9 us
    all_to_all x1, blocking collectives, on_device(): got = lax.all_to_all(sums, ('y', 'c', 'x'), 0, 0, tiled=True)  13.2 us
    all_to_all x1, blocking collectives, on_device(): lax.all_to_all(partial.reshape(4, 64, COMPS * PROBES), 'x', 0, 0, tiled=T...  9.65 us
    pallas_call x8, Pallas kernels, run(): pl.pallas_call(kernel, out_shape=out, in_specs=specs, **kwargs)(*args)  8.21 us
    all_to_all x1, blocking collectives, on_device(): got = lax.all_to_all(sent, 'y', 0, 0, tiled=True)  8.07 us
    all_gather x1, blocking collectives, on_device(): coefficients = lax.all_gather(got, 'c')  6.07 us

profile of v2, /device:TPU:1, one launch (start us, length us, event | category | flops | bytes accessed | tf_op | source)
XLA Modules:
  0.0 118.9 jit_solution(13250960763009174622)
XLA Ops:
  0.6 2.0 %shard_map.94 = bf16[8,72,512]{2,1,0:T(8,128)(2,1)S(1)} custom-call(s32[256,256]{1,0:T(8,128)} %words_ref.3, bf16[64,256]{1,0:T(8,128)(2,1)} %bitcast.9, s32[1,256]{1,0:T(1,128)} %bitcast.10, f32[1,256]{1,0:T(1,128)} %bitcast.13), custom_call_target="tpu_custom_call" | custom-call | tf_op jit(solution)/shard_map/pallas_call | solution.py:316
  2.6 19.5 %all_to_all.35.in_ref = bf16[8,72,512]{2,1,0:T(8,128)(2,1)S(1)} all-to-all(bf16[8,72,512]{2,1,0:T(8,128)(2,1)S(1)} %shard_map.94), channel_id=1, replica_groups=mesh['z'=16,'y'=4,'c'=2,'x'=4] {'y','c'}, dimensions={0} | all-to-all | bytes 1179648 | tf_op jit(solution)/shard_map/all_to_all | solution.py:335
  22.2 0.4 shard_map.95
  22.6 23.1 %all_to_all.36.in_ref = bf16[16,24,128]{2,1,0:T(8,128)(2,1)S(1)} all-to-all(bf16[16,24,128]{2,1,0:T(8,128)(2,1)S(1)} %shard_map.95), channel_id=1, replica_groups=mesh['z'=16,'y'=4,'c'=2,'x'=4] {'z'}, dimensions={0} | all-to-all | bytes 196608 | tf_op jit(solution)/shard_map/all_to_all | solution.py:337
  45.7 1.1 shard_map.96
  46.8 16.4 %all_to_all.37.in_ref = bf16[16,24,128]{2,1,0:T(8,128)(2,1)S(1)} all-to-all(bf16[16,24,128]{2,1,0:T(8,128)(2,1)S(1)} %get-tuple-element.9), channel_id=1, replica_groups=mesh['z'=16,'y'=4,'c'=2,'x'=4] {'z'}, dimensions={0} | all-to-all | bytes 196608 | tf_op jit(solution)/shard_map/all_to_all | solution.py:341
  63.2 0.1 shard_map.97
  63.3 8.1 %all_to_all.38 = bf16[4,72,512]{2,1,0:T(8,128)(2,1)S(1)} all-to-all(bf16[4,72,512]{2,1,0:T(8,128)(2,1)S(1)} %shard_map.97), channel_id=1, replica_groups=mesh['z'=16,'y'=4,'c'=2,'x'=4] {'y'}, dimensions={0} | all-to-all | bytes 589824 | tf_op jit(solution)/shard_map/all_to_all | solution.py:343
  71.4 6.1 %all-gather = bf16[8,72,512]{2,1,0:T(8,128)(2,1)S(1)} all-gather(bf16[4,72,512]{2,1,0:T(8,128)(2,1)S(1)} %all_to_all.38), channel_id=2, replica_groups=mesh['z'=16,'y'=4,'c'=2,'x'=4] {'c'}, dimensions={0}, use_global_device_ids=true | all-gather | bytes 884736 | tf_op jit(solution)/shard_map/all_gather | solution.py:344
  77.5 2.5 %shard_map.98 = bf16[256,512]{1,0:T(8,128)(2,1)S(1)} custom-call(s32[128]{0:T(128)} %comp_ref.1, s32[256,256]{1,0:T(8,128)} %words_ref.3, s32[1,256]{1,0:T(1,128)} %bitcast.11, bf16[2,4,72,512]{3,2,1,0:T(8,128)(2,1)S(1)} %bitcast.7), custom_call_target="tpu_custom_call" | custom-call | tf_op jit(solution)/shard_map/pallas_call | solution.py:316
  80.0 9.7 %all_to_all.39.in_ref = bf16[4,64,512]{2,1,0:T(8,128)(2,1)S(1)} all-to-all(bf16[4,64,512]{2,1,0:T(8,128)(2,1)S(1)} %bitcast.8), channel_id=1, replica_groups=mesh['z'=16,'y'=4,'c'=2,'x'=4] {'x'}, dimensions={0} | all-to-all | bytes 524288 | tf_op jit(solution)/shard_map/all_to_all | solution.py:351
  89.6 1.4 %shard_map.99 = (bf16[64,512]{1,0:T(8,128)(2,1)}, f32[16,1,128]{2,1,0:T(1,128)S(1)}) custom-call(bf16[4,64,512]{2,1,0:T(8,128)(2,1)S(1)} %all_to_all.39.in_ref, f32[8,128]{1,0:T(8,128)S(1)} %get-tuple-element.10.extra_ref, f32[24,128]{1,0:T(8,128)} %constant.4.clone.low_ref, f32[24,128]{1,0:T(8,128)} %constant.5.clone.high_ref), custom_call_target="tpu_custom_call" | custom-call | tf_op jit(solution)/shard_map/pallas_call | solution.py:316
  91.0 13.9 %all_to_all.40.in_ref = f32[16,1,128]{2,1,0:T(1,128)S(1)} all-to-all(f32[16,1,128]{2,1,0:T(1,128)S(1)} %get-tuple-element.12), channel_id=1, replica_groups=mesh['z'=16,'y'=4,'c'=2,'x'=4] {'z'}, dimensions={0} | all-to-all | bytes 16384 | tf_op jit(solution)/shard_map/all_to_all | solution.py:356
  105.0 13.2 %all_to_all.41.in_ref = f32[32,1,128]{2,1,0:T(1,128)S(1)} all-to-all(f32[32,1,128]{2,1,0:T(1,128)S(1)} %shard_map.100), channel_id=1, replica_groups=mesh['z'=16,'y'=4,'c'=2,'x'=4] {'y','c','x'}, dimensions={0} | all-to-all | bytes 32768 | tf_op jit(solution)/shard_map/all_to_all | solution.py:358
  118.2 0.7 shard_map.101
  (1 shorter events, 0.0 us)

commit v3 on v2

--- a/solution.py
+++ b/solution.py
@@ -236,24 +236,33 @@
     acc_ref[...] = jnp.zeros_like(acc_ref)
     words = words_ref[...]
     first_tile = 32 * lax.axis_index("x")
-    for tile in range(32):
+    lane = lax.broadcasted_iota(jnp.int32, (264, 128), 1)
+    blank = jnp.zeros((PROBES, 128), BF16)
+    for tile in range(0, 32, 2):
         y, c = divmod(tile // 4, 2)
         at = 128 * (tile % 4)
-        weights = coef_ref[c, y, :, at : at + 128].astype(F32)
-        x = jnp.concatenate([dosage_tile(words, tile), weights[64:72]], axis=0).astype(BF16)
-        product = dot_nt(x, weights[:64].astype(BF16))
+        weights = coef_ref[c, y, :PROBES, at : at + 256]
+        averages = coef_ref[c, y, PROBES:, at : at + 256].astype(F32)
+        x = jnp.concatenate([dosage_tile(words, tile), dosage_tile(words, tile + 1)], axis=1)
+        x = jnp.concatenate([x, averages], axis=0).astype(BF16)
+        left = jnp.concatenate([weights[:, :128], blank], axis=1)
+        right = jnp.concatenate([blank, weights[:, 128:]], axis=1)
+        product = dot_nt(x, jnp.concatenate([left, right], axis=0))
         comp = comp_ref[first_tile + tile]
-        acc_ref[comp] = acc_ref[comp] + product
+        acc_ref[comp] = acc_ref[comp] + jnp.where(lane < PROBES, product, 0.0)
+        comp = comp_ref[first_tile + tile + 1]
+        acc_ref[comp] = acc_ref[comp] + jnp.where(lane < PROBES, 0.0, product)
     root = jnp.sqrt(counts_ref[...].astype(F32))
     column = jnp.broadcast_to(root, (128, root.shape[1])).T
     for pair in range(4):
         halves = []
         for k in (2 * pair, 2 * pair + 1):
             total = acc_ref[k]
+            total = total + pltpu.roll(total, PROBES, 1)
             centre = total[256:257] + total[257:258] + total[258:259]
             halves.append(total[:256] - centre)
         out_ref[:, 128 * pair : 128 * pair + 128] = (
-            jnp.concatenate(halves, axis=1) * column
+            jnp.where(lane[:256] < PROBES, *halves) * column
         ).astype(BF16)
 
 
@@ -300,7 +309,8 @@
     out_ref[...] = jnp.broadcast_to(jnp.sum(in_ref[...], axis=0, keepdims=True), out_ref.shape)
 
 
-def last_kernel(in_ref, extra_ref, traces_ref, yky_ref):
+def last_kernel(in_ref, extra_ref, held_ref, images_ref, traces_ref, yky_ref):
+    images_ref[...] = held_ref[...]
     sums = jnp.sum(in_ref[...], axis=0)
     weight = extra_ref[1:2]
     scaled = sums * (SNPS / (COMPS * PROBES)) / (weight * weight)
@@ -337,7 +347,7 @@
     got = lax.all_to_all(sent, "z", 0, 0, tiled=True)
     sent, extra = call(
         finish_kernel, (pltpu.VMEM((16, 24, 128), BF16), pltpu.VMEM((8, 128), F32))
-    )(comp_row, near(got))
+    )(near(comp_row), near(got))
     got = lax.all_to_all(sent, "z", 0, 0, tiled=True)
     sent = call(unpack_kernel, pltpu.VMEM((4, ROWS, 512), BF16))(near(got))
     got = lax.all_to_all(sent, "y", 0, 0, tiled=True)
@@ -346,19 +356,20 @@
         images_kernel,
         pltpu.VMEM((256, COMPS * PROBES), BF16),
         scalars=1,
-        scratch_shapes=[pltpu.VMEM((COMPS, 264, PROBES), F32)],
-    )(tile_comp, geno_words, counts_row, near(coefficients))
+        scratch_shapes=[pltpu.VMEM((COMPS, 264, 128), F32)],
+    )(tile_comp, near(geno_words), near(counts_row), near(coefficients))
     pieces = lax.all_to_all(partial.reshape(4, 64, COMPS * PROBES), "x", 0, 0, tiled=True)
     low, high = trace_places()
     images, sums = call(
-        trace_kernel, (shape((64, COMPS * PROBES), BF16), pltpu.VMEM((16, 1, 128), F32))
-    )(near(pieces), near(extra), jnp.asarray(low), jnp.asarray(high))
+        trace_kernel, (pltpu.VMEM((64, COMPS * PROBES), BF16), pltpu.VMEM((16, 1, 128), F32))
+    )(near(pieces), near(extra), near(jnp.asarray(low)), near(jnp.asarray(high)))
     got = lax.all_to_all(sums, "z", 0, 0, tiled=True)
     sums = call(middle_kernel, pltpu.VMEM((32, 1, 128), F32))(near(got))
     got = lax.all_to_all(sums, ("y", "c", "x"), 0, 0, tiled=True)
-    traces, yky = call(last_kernel, (shape((8, 8), F32), shape((1, 8), F32)))(
-        near(got), near(extra)
-    )
+    images, traces, yky = call(
+        last_kernel,
+        (shape((64, COMPS * PROBES), BF16), shape((8, 8), F32), shape((1, 8), F32)),
+    )(near(got), near(extra), near(images))
     return images, traces, yky.reshape(8)
 
 

time: 119 us -> 119 us (level)
  Pallas kernels: 8.21 us -> 6.07 us
  local copies, waits for them, and re-layouts: 0 us -> 1.35 us
    pallas_call x8, Pallas kernels: 8.21 us -> 6.07 us  [run(): pl.pallas_call(kernel, out_shape=out, in_specs=specs, **kwargs)(*args)]
    unnamed x0 -> x10, local copies, waits for them, and re-layouts: none -> 1.35 us
where the time goes in v3:
time: 119 us; the launch traced here: 118 us
  blocking collectives  110 us (92%)
  Pallas kernels  6.07 us (5%)
  local copies, waits for them, and re-layouts  1.35 us (1%)
    all_to_all x2, blocking collectives, on_device(): got = lax.all_to_all(sent, 'z', 0, 0, tiled=True)  39.5 us
    all_to_all x1, blocking collectives, on_device(): got = lax.all_to_all(sent, ('y', 'c'), 0, 0, tiled=True)  19.5 us
    all_to_all x1, blocking collectives, on_device(): got = lax.all_to_all(sums, 'z', 0, 0, tiled=True)  14 us
    all_to_all x1, blocking collectives, on_device(): got = lax.all_to_all(sums, ('y', 'c', 'x'), 0, 0, tiled=True)  13.2 us
    all_to_all x1, blocking collectives, on_device(): lax.all_to_all(partial.reshape(4, 64, COMPS * PROBES), 'x', 0, 0, tiled=T...  9.64 us
    all_to_all x1, blocking collectives, on_device(): got = lax.all_to_all(sent, 'y', 0, 0, tiled=True)  8.07 us
    all_gather x1, blocking collectives, on_device(): coefficients = lax.all_gather(got, 'c')  6.2 us
    pallas_call x8, Pallas kernels, run(): pl.pallas_call(kernel, out_shape=out, in_specs=specs, **kwargs)(*args)  6.07 us

profile of v3, /device:TPU:1, one launch (start us, length us, event | category | flops | bytes accessed | tf_op | source)
XLA Modules:
  0.0 118.2 jit_solution(4566408561067499312)
XLA Ops:
  0.6 2.0 %shard_map.94 = bf16[8,72,512]{2,1,0:T(8,128)(2,1)S(1)} custom-call(s32[256,256]{1,0:T(8,128)} %words_ref.3, bf16[64,256]{1,0:T(8,128)(2,1)} %bitcast.12, s32[1,256]{1,0:T(1,128)} %bitcast.9, f32[1,256]{1,0:T(1,128)} %bitcast.13), custom_call_target="tpu_custom_call" | custom-call | tf_op jit(solution)/shard_map/pallas_call | solution.py:326
  2.6 19.5 %all_to_all.35.in_ref = bf16[8,72,512]{2,1,0:T(8,128)(2,1)S(1)} all-to-all(bf16[8,72,512]{2,1,0:T(8,128)(2,1)S(1)} %shard_map.94), channel_id=1, replica_groups=mesh['z'=16,'y'=4,'c'=2,'x'=4] {'y','c'}, dimensions={0} | all-to-all | bytes 1179648 | tf_op jit(solution)/shard_map/all_to_all | solution.py:345
  22.2 0.4 shard_map.95
  22.6 23.1 %all_to_all.36.in_ref = bf16[16,24,128]{2,1,0:T(8,128)(2,1)S(1)} all-to-all(bf16[16,24,128]{2,1,0:T(8,128)(2,1)S(1)} %shard_map.95), channel_id=1, replica_groups=mesh['z'=16,'y'=4,'c'=2,'x'=4] {'z'}, dimensions={0} | all-to-all | bytes 196608 | tf_op jit(solution)/shard_map/all_to_all | solution.py:347
  45.7 0.0 copy-start.4
  45.7 0.7 copy-done.4
  46.3 0.4 shard_map.96
  46.8 16.4 %all_to_all.37.in_ref = bf16[16,24,128]{2,1,0:T(8,128)(2,1)S(1)} all-to-all(bf16[16,24,128]{2,1,0:T(8,128)(2,1)S(1)} %get-tuple-element.10), channel_id=1, replica_groups=mesh['z'=16,'y'=4,'c'=2,'x'=4] {'z'}, dimensions={0} | all-to-all | bytes 196608 | tf_op jit(solution)/shard_map/all_to_all | solution.py:351
  63.2 0.1 shard_map.97
  63.3 8.1 %all_to_all.38 = bf16[4,72,512]{2,1,0:T(8,128)(2,1)S(1)} all-to-all(bf16[4,72,512]{2,1,0:T(8,128)(2,1)S(1)} %shard_map.97), channel_id=1, replica_groups=mesh['z'=16,'y'=4,'c'=2,'x'=4] {'y'}, dimensions={0} | all-to-all | bytes 589824 | tf_op jit(solution)/shard_map/all_to_all | solution.py:353
  71.4 0.0 copy-start
  71.4 6.2 %all-gather = bf16[8,72,512]{2,1,0:T(8,128)(2,1)S(1)} all-gather(bf16[4,72,512]{2,1,0:T(8,128)(2,1)S(1)} %all_to_all.38), channel_id=2, replica_groups=mesh['z'=16,'y'=4,'c'=2,'x'=4] {'c'}, dimensions={0}, use_global_device_ids=true | all-gather | bytes 884736 | tf_op jit(solution)/shard_map/all_gather | solution.py:354
  77.6 0.0 copy-start.3
  77.6 0.0 copy-done
  77.6 0.7 copy-done.3
  78.3 2.2 %shard_map.98 = bf16[256,512]{1,0:T(8,128)(2,1)S(1)} custom-call(s32[128]{0:T(128)} %comp_ref.1, s32[256,256]{1,0:T(8,128)S(1)} %copy-done, s32[1,256]{1,0:T(1,128)S(1)} %bitcast.10, bf16[2,4,72,512]{3,2,1,0:T(8,128)(2,1)S(1)} %bitcast.7), custom_call_target="tpu_custom_call" | custom-call | tf_op jit(solution)/shard_map/pallas_call | solution.py:326
  80.5 0.0 copy-start.1
  80.5 0.0 copy-start.2
  80.5 9.6 %all_to_all.39.in_ref = bf16[4,64,512]{2,1,0:T(8,128)(2,1)S(1)} all-to-all(bf16[4,64,512]{2,1,0:T(8,128)(2,1)S(1)} %bitcast.8), channel_id=1, replica_groups=mesh['z'=16,'y'=4,'c'=2,'x'=4] {'x'}, dimensions={0} | all-to-all | bytes 524288 | tf_op jit(solution)/shard_map/all_to_all | solution.py:361
  90.1 0.0 copy-done.1
  90.1 0.0 copy-done.2
  90.1 0.2 shard_map.99
  90.4 14.0 %all_to_all.40.in_ref = f32[16,1,128]{2,1,0:T(1,128)S(1)} all-to-all(f32[16,1,128]{2,1,0:T(1,128)S(1)} %get-tuple-element.12), channel_id=1, replica_groups=mesh['z'=16,'y'=4,'c'=2,'x'=4] {'z'}, dimensions={0} | all-to-all | bytes 16384 | tf_op jit(solution)/shard_map/all_to_all | solution.py:366
  104.3 13.2 %all_to_all.41.in_ref = f32[32,1,128]{2,1,0:T(1,128)S(1)} all-to-all(f32[32,1,128]{2,1,0:T(1,128)S(1)} %shard_map.100), channel_id=1, replica_groups=mesh['z'=16,'y'=4,'c'=2,'x'=4] {'y','c','x'}, dimensions={0} | all-to-all | bytes 32768 | tf_op jit(solution)/shard_map/all_to_all | solution.py:368
  117.5 0.7 shard_map.101
  (1 shorter events, 0.0 us)
Async XLA Ops:
  45.7 0.7 copy-start.4
  71.4 6.2 %copy-start = (s32[256,256]{1,0:T(8,128)S(1)}, s32[256,256]{1,0:T(8,128)}, u32[]{:S(2)}) copy-start(s32[256,256]{1,0:T(8,128)} %words_ref.3) | copy-start | bytes 786436
  77.6 0.7 copy-start.3
  80.5 9.7 %copy-start.1 = (f32[24,128]{1,0:T(8,128)S(1)}, f32[24,128]{1,0:T(8,128)}, u32[]{:S(2)}) copy-start(f32[24,128]{1,0:T(8,128)} %constant.5.clone.high_ref) | copy-start | bytes 36868
  80.5 9.7 %copy-start.2 = (f32[24,128]{1,0:T(8,128)S(1)}, f32[24,128]{1,0:T(8,128)}, u32[]{:S(2)}) copy-start(f32[24,128]{1,0:T(8,128)} %constant.4.clone.low_ref) | copy-start | bytes 36868

commit v4 on v3

--- a/solution.py
+++ b/solution.py
@@ -62,9 +62,16 @@
     return (lax.shift_right_logical(block, jnp.int32(2 * field)) & 3).astype(F32)
 
 
-def panel_kernel(words_ref, probes_ref, counts_ref, pheno_ref, out_ref):
+def panel_kernel(
+    comp_ref, words_ref, probes_ref, counts_ref, pheno_ref, comps_ref, out_ref, root_ref, held_ref, own_ref
+):
+    held_ref[...] = comps_ref[...]
+    first_tile = 32 * lax.axis_index("x")
+    for tile in range(32):
+        own_ref[tile] = comp_ref[first_tile + tile]
     counts = counts_ref[...].astype(F32)
     root = jnp.sqrt(counts)
+    root_ref[...] = root
     probe_rows = rounded(probes_ref[...].astype(F32) * root)
     pheno_rows = rounded(pheno_ref[...] * root)
     tail = stacked([pheno_rows, counts], 64)
@@ -79,8 +86,9 @@
     words = words_ref[...]
     for group in range(8):
         x = jnp.concatenate([dosage_tile(words, 4 * group + i) for i in range(4)], axis=1)
-        sums = jnp.dot(left, x.astype(BF16), preferred_element_type=F32)
-        squares = jnp.dot(left_tail, (x * x).astype(BF16), preferred_element_type=F32)[1:2]
+        x = x.astype(BF16)
+        sums = jnp.dot(left, x, preferred_element_type=F32)
+        squares = jnp.dot(left_tail, x * x, preferred_element_type=F32)[1:2]
         first = sums[COUNT : COUNT + 1]
         centre = rounded(first * rate)
         centred = sums - column * centre
@@ -232,10 +240,9 @@
             out_ref[d, :, 128 * tile : 128 * tile + 128] = whole
 
 
-def images_kernel(comp_ref, words_ref, counts_ref, coef_ref, out_ref, acc_ref):
+def images_kernel(comp_ref, words_ref, root_ref, coef_ref, out_ref, acc_ref):
     acc_ref[...] = jnp.zeros_like(acc_ref)
     words = words_ref[...]
-    first_tile = 32 * lax.axis_index("x")
     lane = lax.broadcasted_iota(jnp.int32, (264, 128), 1)
     blank = jnp.zeros((PROBES, 128), BF16)
     for tile in range(0, 32, 2):
@@ -248,12 +255,11 @@
         left = jnp.concatenate([weights[:, :128], blank], axis=1)
         right = jnp.concatenate([blank, weights[:, 128:]], axis=1)
         product = dot_nt(x, jnp.concatenate([left, right], axis=0))
-        comp = comp_ref[first_tile + tile]
+        comp = comp_ref[tile]
         acc_ref[comp] = acc_ref[comp] + jnp.where(lane < PROBES, product, 0.0)
-        comp = comp_ref[first_tile + tile + 1]
+        comp = comp_ref[tile + 1]
         acc_ref[comp] = acc_ref[comp] + jnp.where(lane < PROBES, 0.0, product)
-    root = jnp.sqrt(counts_ref[...].astype(F32))
-    column = jnp.broadcast_to(root, (128, root.shape[1])).T
+    column = jnp.broadcast_to(root_ref[...], (128, root_ref.shape[1])).T
     for pair in range(4):
         halves = []
         for k in (2 * pair, 2 * pair + 1):
@@ -337,17 +343,32 @@
 
 
 def on_device(geno_words, counts, probes, phenotype, tile_comp):
-    counts_row = counts.reshape(1, -1)
     comp_row = tile_comp.reshape(1, -1)
-    sent = call(panel_kernel, pltpu.VMEM((8, ROWS, 512), BF16))(
-        geno_words, probes.T, counts_row, phenotype.reshape(1, -1)
+    sent, root, comps, own_comps = call(
+        panel_kernel,
+        [
+            pltpu.VMEM((8, ROWS, 512), BF16),
+            pltpu.VMEM((1, 256), F32),
+            pltpu.VMEM((1, 128), jnp.int32),
+            pltpu.SMEM((32,), jnp.int32),
+        ],
+        scalars=1,
+        out_specs=[pl.BlockSpec(memory_space=pltpu.VMEM)] * 3
+        + [pl.BlockSpec(memory_space=pltpu.SMEM)],
+    )(
+        tile_comp,
+        geno_words,
+        probes.T,
+        counts.reshape(1, -1),
+        phenotype.reshape(1, -1),
+        comp_row,
     )
     got = lax.all_to_all(sent, ("y", "c"), 0, 0, tiled=True)
     sent = call(regroup_kernel, pltpu.VMEM((16, 24, 128), BF16))(near(got))
     got = lax.all_to_all(sent, "z", 0, 0, tiled=True)
     sent, extra = call(
         finish_kernel, (pltpu.VMEM((16, 24, 128), BF16), pltpu.VMEM((8, 128), F32))
-    )(near(comp_row), near(got))
+    )(near(comps), near(got))
     got = lax.all_to_all(sent, "z", 0, 0, tiled=True)
     sent = call(unpack_kernel, pltpu.VMEM((4, ROWS, 512), BF16))(near(got))
     got = lax.all_to_all(sent, "y", 0, 0, tiled=True)
@@ -357,7 +378,12 @@
         pltpu.VMEM((256, COMPS * PROBES), BF16),
         scalars=1,
         scratch_shapes=[pltpu.VMEM((COMPS, 264, 128), F32)],
-    )(tile_comp, near(geno_words), near(counts_row), near(coefficients))
+    )(
+        pltpu.with_memory_space_constraint(own_comps, pltpu.SMEM),
+        near(geno_words),
+        near(root),
+        near(coefficients),
+    )
     pieces = lax.all_to_all(partial.reshape(4, 64, COMPS * PROBES), "x", 0, 0, tiled=True)
     low, high = trace_places()
     images, sums = call(

time: 119 us -> 117 us (0.983)
  local copies, waits for them, and re-layouts: 1.35 us -> 0.02 us
    unnamed x10 -> x6, local copies, waits for them, and re-layouts: 1.35 us -> 0.02 us
where the time goes in v4:
time: 117 us; the launch traced here: 116 us
  blocking collectives  110 us (94%)
  Pallas kernels  5.28 us (5%)
    all_to_all x2, blocking collectives, on_device(): got = lax.all_to_all(sent, 'z', 0, 0, tiled=True)  39.5 us
    all_to_all x1, blocking collectives, on_device(): got = lax.all_to_all(sent, ('y', 'c'), 0, 0, tiled=True)  19.5 us
    all_to_all x1, blocking collectives, on_device(): got = lax.all_to_all(sums, 'z', 0, 0, tiled=True)  14 us
    all_to_all x1, blocking collectives, on_device(): got = lax.all_to_all(sums, ('y', 'c', 'x'), 0, 0, tiled=True)  13.2 us
    all_to_all x1, blocking collectives, on_device(): lax.all_to_all(partial.reshape(4, 64, COMPS * PROBES), 'x', 0, 0, tiled=T...  9.66 us
    all_to_all x1, blocking collectives, on_device(): got = lax.all_to_all(sent, 'y', 0, 0, tiled=True)  8.07 us
    all_gather x1, blocking collectives, on_device(): coefficients = lax.all_gather(got, 'c')  6.2 us
    pallas_call x8, Pallas kernels, run(): pl.pallas_call(kernel, out_shape=out, in_specs=specs, **kwargs)(*args)  5.28 us

profile of v4, /device:TPU:1, one launch (start us, length us, event | category | flops | bytes accessed | tf_op | source)
XLA Modules:
  0.0 116.1 jit_solution(3344174953594461820)
XLA Ops:
  0.6 1.9 %shard_map.94 = (bf16[8,72,512]{2,1,0:T(8,128)(2,1)S(1)}, f32[1,256]{1,0:T(1,128)S(1)}, s32[1,128]{1,0:T(1,128)S(1)}, s32[32]{0:T(128)S(4)}) custom-call(s32[128]{0:T(128)} %comp_ref.1, s32[256,256]{1,0:T(8,128)} %words_ref.3, bf16[64,256]{1,0:T(8,128)(2,1)} %bitcast.9, s32[1,256]{1,0:T(1,128)} %bitcast.11, f32[1,256]{1,0:T(1,128)} %bitcast.12, ...), custom_call_target="tpu_custom_call" | custom-call | tf_op jit(solution)/shard_map/pallas_call | solution.py:332
  2.5 19.5 %all_to_all.35.in_ref = bf16[8,72,512]{2,1,0:T(8,128)(2,1)S(1)} all-to-all(bf16[8,72,512]{2,1,0:T(8,128)(2,1)S(1)} %get-tuple-element.17), channel_id=1, replica_groups=mesh['z'=16,'y'=4,'c'=2,'x'=4] {'y','c'}, dimensions={0} | all-to-all | bytes 1179648 | tf_op jit(solution)/shard_map/all_to_all | solution.py:366
  22.1 0.4 shard_map.95
  22.5 23.1 %all_to_all.36.in_ref = bf16[16,24,128]{2,1,0:T(8,128)(2,1)S(1)} all-to-all(bf16[16,24,128]{2,1,0:T(8,128)(2,1)S(1)} %shard_map.95), channel_id=1, replica_groups=mesh['z'=16,'y'=4,'c'=2,'x'=4] {'z'}, dimensions={0} | all-to-all | bytes 196608 | tf_op jit(solution)/shard_map/all_to_all | solution.py:368
  45.6 0.4 shard_map.96
  46.0 16.4 %all_to_all.37.in_ref = bf16[16,24,128]{2,1,0:T(8,128)(2,1)S(1)} all-to-all(bf16[16,24,128]{2,1,0:T(8,128)(2,1)S(1)} %get-tuple-element.18), channel_id=1, replica_groups=mesh['z'=16,'y'=4,'c'=2,'x'=4] {'z'}, dimensions={0} | all-to-all | bytes 196608 | tf_op jit(solution)/shard_map/all_to_all | solution.py:372
  62.4 0.1 shard_map.97
  62.6 8.1 %all_to_all.38 = bf16[4,72,512]{2,1,0:T(8,128)(2,1)S(1)} all-to-all(bf16[4,72,512]{2,1,0:T(8,128)(2,1)S(1)} %shard_map.97), channel_id=1, replica_groups=mesh['z'=16,'y'=4,'c'=2,'x'=4] {'y'}, dimensions={0} | all-to-all | bytes 589824 | tf_op jit(solution)/shard_map/all_to_all | solution.py:374
  70.6 0.0 copy-start
  70.6 6.2 %all-gather = bf16[8,72,512]{2,1,0:T(8,128)(2,1)S(1)} all-gather(bf16[4,72,512]{2,1,0:T(8,128)(2,1)S(1)} %all_to_all.38), channel_id=2, replica_groups=mesh['z'=16,'y'=4,'c'=2,'x'=4] {'c'}, dimensions={0}, use_global_device_ids=true | all-gather | bytes 884736 | tf_op jit(solution)/shard_map/all_gather | solution.py:375
  76.8 0.0 copy-done
  76.8 1.5 %shard_map.98 = bf16[256,512]{1,0:T(8,128)(2,1)S(1)} custom-call(s32[32]{0:T(128)S(4)} %get-tuple-element.14.comp_ref, s32[256,256]{1,0:T(8,128)S(1)} %copy-done, f32[1,256]{1,0:T(1,128)S(1)} %get-tuple-element.15.root_ref, bf16[2,4,72,512]{3,2,1,0:T(8,128)(2,1)S(1)} %bitcast.7), custom_call_target="tpu_custom_call" | custom-call | tf_op jit(solution)/shard_map/pallas_call | solution.py:332
  78.3 0.0 copy-start.1
  78.4 0.0 copy-start.2
  78.4 9.7 %all_to_all.39.in_ref = bf16[4,64,512]{2,1,0:T(8,128)(2,1)S(1)} all-to-all(bf16[4,64,512]{2,1,0:T(8,128)(2,1)S(1)} %bitcast.8), channel_id=1, replica_groups=mesh['z'=16,'y'=4,'c'=2,'x'=4] {'x'}, dimensions={0} | all-to-all | bytes 524288 | tf_op jit(solution)/shard_map/all_to_all | solution.py:387
  88.0 0.0 copy-done.1
  88.0 0.0 copy-done.2
  88.0 0.2 shard_map.99
  88.2 14.0 %all_to_all.40.in_ref = f32[16,1,128]{2,1,0:T(1,128)S(1)} all-to-all(f32[16,1,128]{2,1,0:T(1,128)S(1)} %get-tuple-element.20), channel_id=1, replica_groups=mesh['z'=16,'y'=4,'c'=2,'x'=4] {'z'}, dimensions={0} | all-to-all | bytes 16384 | tf_op jit(solution)/shard_map/all_to_all | solution.py:392
  102.2 13.2 %all_to_all.41.in_ref = f32[32,1,128]{2,1,0:T(1,128)S(1)} all-to-all(f32[32,1,128]{2,1,0:T(1,128)S(1)} %shard_map.100), channel_id=1, replica_groups=mesh['z'=16,'y'=4,'c'=2,'x'=4] {'y','c','x'}, dimensions={0} | all-to-all | bytes 32768 | tf_op jit(solution)/shard_map/all_to_all | solution.py:394
  115.4 0.7 shard_map.101
  (1 shorter events, 0.0 us)
Async XLA Ops:
  70.6 6.2 %copy-start = (s32[256,256]{1,0:T(8,128)S(1)}, s32[256,256]{1,0:T(8,128)}, u32[]{:S(2)}) copy-start(s32[256,256]{1,0:T(8,128)} %words_ref.3) | copy-start | bytes 786436
  78.3 9.7 %copy-start.1 = (f32[24,128]{1,0:T(8,128)S(1)}, f32[24,128]{1,0:T(8,128)}, u32[]{:S(2)}) copy-start(f32[24,128]{1,0:T(8,128)} %constant.5.clone.high_ref) | copy-start | bytes 36868
  78.4 9.7 %copy-start.2 = (f32[24,128]{1,0:T(8,128)S(1)}, f32[24,128]{1,0:T(8,128)}, u32[]{:S(2)}) copy-start(f32[24,128]{1,0:T(8,128)} %constant.4.clone.low_ref) | copy-start | bytes 36868

commit v5 on v4

--- a/solution.py
+++ b/solution.py
@@ -387,11 +387,11 @@
     pieces = lax.all_to_all(partial.reshape(4, 64, COMPS * PROBES), "x", 0, 0, tiled=True)
     low, high = trace_places()
     images, sums = call(
-        trace_kernel, (pltpu.VMEM((64, COMPS * PROBES), BF16), pltpu.VMEM((16, 1, 128), F32))
+        trace_kernel, (pltpu.VMEM((64, COMPS * PROBES), BF16), pltpu.VMEM((32, 1, 128), F32))
     )(near(pieces), near(extra), near(jnp.asarray(low)), near(jnp.asarray(high)))
+    got = lax.all_to_all(sums, ("y", "c", "x"), 0, 0, tiled=True)
+    sums = call(middle_kernel, pltpu.VMEM((16, 1, 128), F32))(near(got))
     got = lax.all_to_all(sums, "z", 0, 0, tiled=True)
-    sums = call(middle_kernel, pltpu.VMEM((32, 1, 128), F32))(near(got))
-    got = lax.all_to_all(sums, ("y", "c", "x"), 0, 0, tiled=True)
     images, traces, yky = call(
         last_kernel,
         (shape((64, COMPS * PROBES), BF16), shape((8, 8), F32), shape((1, 8), F32)),

time: 117 us -> 115 us (0.983)
    all_to_all x1, blocking collectives: 13.2 us -> 11.8 us  [on_device(): got = lax.all_to_all(sums, ('y', 'c', 'x'), 0, 0, tiled=True)]
where the time goes in v5:
time: 115 us
  blocking collectives  109 us (95%)
  Pallas kernels  5.28 us (5%)
    all_to_all x2, blocking collectives, on_device(): got = lax.all_to_all(sent, 'z', 0, 0, tiled=True)  39.5 us
    all_to_all x1, blocking collectives, on_device(): got = lax.all_to_all(sent, ('y', 'c'), 0, 0, tiled=True)  19.5 us
    all_to_all x1, blocking collectives, on_device(): got = lax.all_to_all(sums, 'z', 0, 0, tiled=True)  14 us
    all_to_all x1, blocking collectives, on_device(): got = lax.all_to_all(sums, ('y', 'c', 'x'), 0, 0, tiled=True)  11.8 us
    all_to_all x1, blocking collectives, on_device(): lax.all_to_all(partial.reshape(4, 64, COMPS * PROBES), 'x', 0, 0, tiled=T...  9.64 us
    all_to_all x1, blocking collectives, on_device(): got = lax.all_to_all(sent, 'y', 0, 0, tiled=True)  8.07 us
    all_gather x1, blocking collectives, on_device(): coefficients = lax.all_gather(got, 'c')  6.2 us
    pallas_call x8, Pallas kernels, run(): pl.pallas_call(kernel, out_shape=out, in_specs=specs, **kwargs)(*args)  5.28 us

profile of v5, /device:TPU:1, one launch (start us, length us, event | category | flops | bytes accessed | tf_op | source)
XLA Modules:
  0.0 114.7 jit_solution(12283097587264433561)
XLA Ops:
  0.6 1.9 %shard_map.94 = (bf16[8,72,512]{2,1,0:T(8,128)(2,1)S(1)}, f32[1,256]{1,0:T(1,128)S(1)}, s32[1,128]{1,0:T(1,128)S(1)}, s32[32]{0:T(128)S(4)}) custom-call(s32[128]{0:T(128)} %comp_ref.1, s32[256,256]{1,0:T(8,128)} %words_ref.3, bf16[64,256]{1,0:T(8,128)(2,1)} %bitcast.9, s32[1,256]{1,0:T(1,128)} %bitcast.11, f32[1,256]{1,0:T(1,128)} %bitcast.12, ...), custom_call_target="tpu_custom_call" | custom-call | tf_op jit(solution)/shard_map/pallas_call | solution.py:332
  2.5 19.5 %all_to_all.35.in_ref = bf16[8,72,512]{2,1,0:T(8,128)(2,1)S(1)} all-to-all(bf16[8,72,512]{2,1,0:T(8,128)(2,1)S(1)} %get-tuple-element.17), channel_id=1, replica_groups=mesh['z'=16,'y'=4,'c'=2,'x'=4] {'y','c'}, dimensions={0} | all-to-all | bytes 1179648 | tf_op jit(solution)/shard_map/all_to_all | solution.py:366
  22.1 0.4 shard_map.95
  22.5 23.1 %all_to_all.36.in_ref = bf16[16,24,128]{2,1,0:T(8,128)(2,1)S(1)} all-to-all(bf16[16,24,128]{2,1,0:T(8,128)(2,1)S(1)} %shard_map.95), channel_id=1, replica_groups=mesh['z'=16,'y'=4,'c'=2,'x'=4] {'z'}, dimensions={0} | all-to-all | bytes 196608 | tf_op jit(solution)/shard_map/all_to_all | solution.py:368
  45.6 0.4 shard_map.96
  46.0 16.4 %all_to_all.37.in_ref = bf16[16,24,128]{2,1,0:T(8,128)(2,1)S(1)} all-to-all(bf16[16,24,128]{2,1,0:T(8,128)(2,1)S(1)} %get-tuple-element.18), channel_id=1, replica_groups=mesh['z'=16,'y'=4,'c'=2,'x'=4] {'z'}, dimensions={0} | all-to-all | bytes 196608 | tf_op jit(solution)/shard_map/all_to_all | solution.py:372
  62.4 0.1 shard_map.97
  62.6 8.1 %all_to_all.38 = bf16[4,72,512]{2,1,0:T(8,128)(2,1)S(1)} all-to-all(bf16[4,72,512]{2,1,0:T(8,128)(2,1)S(1)} %shard_map.97), channel_id=1, replica_groups=mesh['z'=16,'y'=4,'c'=2,'x'=4] {'y'}, dimensions={0} | all-to-all | bytes 589824 | tf_op jit(solution)/shard_map/all_to_all | solution.py:374
  70.6 0.0 copy-start
  70.6 6.2 %all-gather = bf16[8,72,512]{2,1,0:T(8,128)(2,1)S(1)} all-gather(bf16[4,72,512]{2,1,0:T(8,128)(2,1)S(1)} %all_to_all.38), channel_id=2, replica_groups=mesh['z'=16,'y'=4,'c'=2,'x'=4] {'c'}, dimensions={0}, use_global_device_ids=true | all-gather | bytes 884736 | tf_op jit(solution)/shard_map/all_gather | solution.py:375
  76.8 0.0 copy-done
  76.8 1.5 %shard_map.98 = bf16[256,512]{1,0:T(8,128)(2,1)S(1)} custom-call(s32[32]{0:T(128)S(4)} %get-tuple-element.14.comp_ref, s32[256,256]{1,0:T(8,128)S(1)} %copy-done, f32[1,256]{1,0:T(1,128)S(1)} %get-tuple-element.15.root_ref, bf16[2,4,72,512]{3,2,1,0:T(8,128)(2,1)S(1)} %bitcast.7), custom_call_target="tpu_custom_call" | custom-call | tf_op jit(solution)/shard_map/pallas_call | solution.py:332
  78.3 0.0 copy-start.1
  78.4 0.0 copy-start.2
  78.4 9.6 %all_to_all.39.in_ref = bf16[4,64,512]{2,1,0:T(8,128)(2,1)S(1)} all-to-all(bf16[4,64,512]{2,1,0:T(8,128)(2,1)S(1)} %bitcast.8), channel_id=1, replica_groups=mesh['z'=16,'y'=4,'c'=2,'x'=4] {'x'}, dimensions={0} | all-to-all | bytes 524288 | tf_op jit(solution)/shard_map/all_to_all | solution.py:387
  88.0 0.0 copy-done.1
  88.0 0.0 copy-done.2
  88.0 0.2 shard_map.99
  88.2 11.8 %all_to_all.40.in_ref = f32[32,1,128]{2,1,0:T(1,128)S(1)} all-to-all(f32[32,1,128]{2,1,0:T(1,128)S(1)} %get-tuple-element.20), channel_id=1, replica_groups=mesh['z'=16,'y'=4,'c'=2,'x'=4] {'y','c','x'}, dimensions={0} | all-to-all | bytes 32768 | tf_op jit(solution)/shard_map/all_to_all | solution.py:392
  100.0 14.0 %all_to_all.41.in_ref = f32[16,1,128]{2,1,0:T(1,128)S(1)} all-to-all(f32[16,1,128]{2,1,0:T(1,128)S(1)} %shard_map.100), channel_id=1, replica_groups=mesh['z'=16,'y'=4,'c'=2,'x'=4] {'z'}, dimensions={0} | all-to-all | bytes 16384 | tf_op jit(solution)/shard_map/all_to_all | solution.py:394
  114.0 0.7 shard_map.101
  (1 shorter events, 0.0 us)
Async XLA Ops:
  70.6 6.2 %copy-start = (s32[256,256]{1,0:T(8,128)S(1)}, s32[256,256]{1,0:T(8,128)}, u32[]{:S(2)}) copy-start(s32[256,256]{1,0:T(8,128)} %words_ref.3) | copy-start | bytes 786436
  78.3 9.7 %copy-start.1 = (f32[24,128]{1,0:T(8,128)S(1)}, f32[24,128]{1,0:T(8,128)}, u32[]{:S(2)}) copy-start(f32[24,128]{1,0:T(8,128)} %constant.5.clone.high_ref) | copy-start | bytes 36868
  78.4 9.7 %copy-start.2 = (f32[24,128]{1,0:T(8,128)S(1)}, f32[24,128]{1,0:T(8,128)}, u32[]{:S(2)}) copy-start(f32[24,128]{1,0:T(8,128)} %constant.4.clone.low_ref) | copy-start | bytes 36868

commit v6 on v5

--- a/solution.py
+++ b/solution.py
@@ -240,36 +240,33 @@
             out_ref[d, :, 128 * tile : 128 * tile + 128] = whole
 
 
-def images_kernel(comp_ref, words_ref, root_ref, coef_ref, out_ref, acc_ref):
+def images_kernel(comp_ref, words_ref, root_ref, coef_ref, out_ref, acc_ref, centre_ref):
     acc_ref[...] = jnp.zeros_like(acc_ref)
+    centre_ref[...] = jnp.zeros_like(centre_ref)
     words = words_ref[...]
-    lane = lax.broadcasted_iota(jnp.int32, (264, 128), 1)
     blank = jnp.zeros((PROBES, 128), BF16)
-    for tile in range(0, 32, 2):
-        y, c = divmod(tile // 4, 2)
-        at = 128 * (tile % 4)
+    for pair in range(0, 32, 2):
+        y, c = divmod(pair // 4, 2)
+        at = 128 * (pair % 4)
         weights = coef_ref[c, y, :PROBES, at : at + 256]
         averages = coef_ref[c, y, PROBES:, at : at + 256].astype(F32)
-        x = jnp.concatenate([dosage_tile(words, tile), dosage_tile(words, tile + 1)], axis=1)
-        x = jnp.concatenate([x, averages], axis=0).astype(BF16)
+        average = averages[0:1] + averages[1:2] + averages[2:3]
+        x = jnp.concatenate([dosage_tile(words, pair), dosage_tile(words, pair + 1)], axis=1)
         left = jnp.concatenate([weights[:, :128], blank], axis=1)
         right = jnp.concatenate([blank, weights[:, 128:]], axis=1)
-        product = dot_nt(x, jnp.concatenate([left, right], axis=0))
-        comp = comp_ref[tile]
-        acc_ref[comp] = acc_ref[comp] + jnp.where(lane < PROBES, product, 0.0)
-        comp = comp_ref[tile + 1]
-        acc_ref[comp] = acc_ref[comp] + jnp.where(lane < PROBES, 0.0, product)
-    column = jnp.broadcast_to(root_ref[...], (128, root_ref.shape[1])).T
+        product = dot_nt(jnp.concatenate([left, right], axis=0), x.astype(BF16))
+        shares = weights.astype(F32) * average
+        for i in range(2):
+            comp = comp_ref[pair + i]
+            acc_ref[comp] = acc_ref[comp] + product[PROBES * i : PROBES * i + PROBES]
+            centre_ref[comp] = centre_ref[comp] + shares[:, 128 * i : 128 * i + 128]
+    root = root_ref[...]
     for pair in range(4):
         halves = []
         for k in (2 * pair, 2 * pair + 1):
-            total = acc_ref[k]
-            total = total + pltpu.roll(total, PROBES, 1)
-            centre = total[256:257] + total[257:258] + total[258:259]
-            halves.append(total[:256] - centre)
-        out_ref[:, 128 * pair : 128 * pair + 128] = (
-            jnp.where(lane[:256] < PROBES, *halves) * column
-        ).astype(BF16)
+            centre = jnp.sum(centre_ref[k], axis=1, keepdims=True)
+            halves.append((acc_ref[k] - centre) * root)
+        out_ref[:, 128 * pair : 128 * pair + 128] = jnp.concatenate(halves, axis=0).T.astype(BF16)
 
 
 def trace_places():
@@ -377,7 +374,10 @@
         images_kernel,
         pltpu.VMEM((256, COMPS * PROBES), BF16),
         scalars=1,
-        scratch_shapes=[pltpu.VMEM((COMPS, 264, 128), F32)],
+        scratch_shapes=[
+            pltpu.VMEM((COMPS, PROBES, 256), F32),
+            pltpu.VMEM((COMPS, PROBES, 128), F32),
+        ],
     )(
         pltpu.with_memory_space_constraint(own_comps, pltpu.SMEM),
         near(geno_words),

time: 115 us -> 115 us (level)
  no operation moved by 1% of the time
where the time goes in v6:
time: 115 us; the launch traced here: 114 us
  blocking collectives  109 us (95%)
  Pallas kernels  4.91 us (4%)
    all_to_all x2, blocking collectives, on_device(): got = lax.all_to_all(sent, 'z', 0, 0, tiled=True)  39.5 us
    all_to_all x1, blocking collectives, on_device(): got = lax.all_to_all(sent, ('y', 'c'), 0, 0, tiled=True)  19.5 us
    all_to_all x1, blocking collectives, on_device(): got = lax.all_to_all(sums, 'z', 0, 0, tiled=True)  14 us
    all_to_all x1, blocking collectives, on_device(): got = lax.all_to_all(sums, ('y', 'c', 'x'), 0, 0, tiled=True)  11.8 us
    all_to_all x1, blocking collectives, on_device(): lax.all_to_all(partial.reshape(4, 64, COMPS * PROBES), 'x', 0, 0, tiled=T...  9.63 us
    all_to_all x1, blocking collectives, on_device(): got = lax.all_to_all(sent, 'y', 0, 0, tiled=True)  8.07 us
    all_gather x1, blocking collectives, on_device(): coefficients = lax.all_gather(got, 'c')  6.2 us
    pallas_call x8, Pallas kernels, run(): pl.pallas_call(kernel, out_shape=out, in_specs=specs, **kwargs)(*args)  4.91 us

profile of v6, /device:TPU:1, one launch (start us, length us, event | category | flops | bytes accessed | tf_op | source)
XLA Modules:
  0.0 114.3 jit_solution(3865072929528388062)
XLA Ops:
  0.6 1.9 %shard_map.94 = (bf16[8,72,512]{2,1,0:T(8,128)(2,1)S(1)}, f32[1,256]{1,0:T(1,128)S(1)}, s32[1,128]{1,0:T(1,128)S(1)}, s32[32]{0:T(128)S(4)}) custom-call(s32[128]{0:T(128)} %comp_ref.1, s32[256,256]{1,0:T(8,128)} %words_ref.3, bf16[64,256]{1,0:T(8,128)(2,1)} %bitcast.9, s32[1,256]{1,0:T(1,128)} %bitcast.11, f32[1,256]{1,0:T(1,128)} %bitcast.12, ...), custom_call_target="tpu_custom_call" | custom-call | tf_op jit(solution)/shard_map/pallas_call | solution.py:329
  2.5 19.5 %all_to_all.35.in_ref = bf16[8,72,512]{2,1,0:T(8,128)(2,1)S(1)} all-to-all(bf16[8,72,512]{2,1,0:T(8,128)(2,1)S(1)} %get-tuple-element.17), channel_id=1, replica_groups=mesh['z'=16,'y'=4,'c'=2,'x'=4] {'y','c'}, dimensions={0} | all-to-all | bytes 1179648 | tf_op jit(solution)/shard_map/all_to_all | solution.py:363
  22.1 0.4 shard_map.95
  22.5 23.1 %all_to_all.36.in_ref = bf16[16,24,128]{2,1,0:T(8,128)(2,1)S(1)} all-to-all(bf16[16,24,128]{2,1,0:T(8,128)(2,1)S(1)} %shard_map.95), channel_id=1, replica_groups=mesh['z'=16,'y'=4,'c'=2,'x'=4] {'z'}, dimensions={0} | all-to-all | bytes 196608 | tf_op jit(solution)/shard_map/all_to_all | solution.py:365
  45.6 0.4 shard_map.96
  46.0 16.4 %all_to_all.37.in_ref = bf16[16,24,128]{2,1,0:T(8,128)(2,1)S(1)} all-to-all(bf16[16,24,128]{2,1,0:T(8,128)(2,1)S(1)} %get-tuple-element.18), channel_id=1, replica_groups=mesh['z'=16,'y'=4,'c'=2,'x'=4] {'z'}, dimensions={0} | all-to-all | bytes 196608 | tf_op jit(solution)/shard_map/all_to_all | solution.py:369
  62.4 0.1 shard_map.97
  62.6 8.1 %all_to_all.38 = bf16[4,72,512]{2,1,0:T(8,128)(2,1)S(1)} all-to-all(bf16[4,72,512]{2,1,0:T(8,128)(2,1)S(1)} %shard_map.97), channel_id=1, replica_groups=mesh['z'=16,'y'=4,'c'=2,'x'=4] {'y'}, dimensions={0} | all-to-all | bytes 589824 | tf_op jit(solution)/shard_map/all_to_all | solution.py:371
  70.6 0.0 copy-start
  70.6 6.2 %all-gather = bf16[8,72,512]{2,1,0:T(8,128)(2,1)S(1)} all-gather(bf16[4,72,512]{2,1,0:T(8,128)(2,1)S(1)} %all_to_all.38), channel_id=2, replica_groups=mesh['z'=16,'y'=4,'c'=2,'x'=4] {'c'}, dimensions={0}, use_global_device_ids=true | all-gather | bytes 884736 | tf_op jit(solution)/shard_map/all_gather | solution.py:372
  76.8 0.0 copy-done
  76.8 1.1 shard_map.98
  78.0 0.0 copy-start.1
  78.0 0.0 copy-start.2
  78.0 9.6 %all_to_all.39.in_ref = bf16[4,64,512]{2,1,0:T(8,128)(2,1)S(1)} all-to-all(bf16[4,64,512]{2,1,0:T(8,128)(2,1)S(1)} %bitcast.8), channel_id=1, replica_groups=mesh['z'=16,'y'=4,'c'=2,'x'=4] {'x'}, dimensions={0} | all-to-all | bytes 524288 | tf_op jit(solution)/shard_map/all_to_all | solution.py:387
  87.6 0.0 copy-done.1
  87.6 0.0 copy-done.2
  87.6 0.2 shard_map.99
  87.9 11.8 %all_to_all.40.in_ref = f32[32,1,128]{2,1,0:T(1,128)S(1)} all-to-all(f32[32,1,128]{2,1,0:T(1,128)S(1)} %get-tuple-element.20), channel_id=1, replica_groups=mesh['z'=16,'y'=4,'c'=2,'x'=4] {'y','c','x'}, dimensions={0} | all-to-all | bytes 32768 | tf_op jit(solution)/shard_map/all_to_all | solution.py:392
  99.7 14.0 %all_to_all.41.in_ref = f32[16,1,128]{2,1,0:T(1,128)S(1)} all-to-all(f32[16,1,128]{2,1,0:T(1,128)S(1)} %shard_map.100), channel_id=1, replica_groups=mesh['z'=16,'y'=4,'c'=2,'x'=4] {'z'}, dimensions={0} | all-to-all | bytes 16384 | tf_op jit(solution)/shard_map/all_to_all | solution.py:394
  113.6 0.7 shard_map.101
  (1 shorter events, 0.0 us)
Async XLA Ops:
  70.6 6.2 %copy-start = (s32[256,256]{1,0:T(8,128)S(1)}, s32[256,256]{1,0:T(8,128)}, u32[]{:S(2)}) copy-start(s32[256,256]{1,0:T(8,128)} %words_ref.3) | copy-start | bytes 786436
  78.0 9.7 %copy-start.1 = (f32[24,128]{1,0:T(8,128)S(1)}, f32[24,128]{1,0:T(8,128)}, u32[]{:S(2)}) copy-start(f32[24,128]{1,0:T(8,128)} %constant.5.clone.high_ref) | copy-start | bytes 36868
  78.0 9.6 %copy-start.2 = (f32[24,128]{1,0:T(8,128)S(1)}, f32[24,128]{1,0:T(8,128)}, u32[]{:S(2)}) copy-start(f32[24,128]{1,0:T(8,128)} %constant.4.clone.low_ref) | copy-start | bytes 36868
